TPU v7x, 8 devices: a whole 2x2x1 slice. The times are simulated.
8 devices in a mesh: rep: 1 (over z), dp: 8 (over x, y, core).
Axes of the slice: x: 2, y: 2, z: 1, core: 2. Of those that a mesh axis runs over, the one named last changes fastest.
Arguments:
- x: bfloat16 [8, 2048, 1152], P(('rep', 'dp'))
- dy: bfloat16 [8, 2048, 1152], P(('rep', 'dp'))
- w_gate: bfloat16 [2, 1152, 4608], P(None, 'dp')
- w_up: bfloat16 [2, 1152, 4608], P(None, 'dp')
- w_down: bfloat16 [2, 4608, 1152], P(None, 'dp')
Outputs:
- output 1: bfloat16 [8, 2048, 1152], P(('rep', 'dp'))
- output 2: bfloat16 [2, 1152, 4608], P('rep', 'dp')
- output 3: bfloat16 [2, 1152, 4608], P('rep', 'dp')
- output 4: bfloat16 [2, 4608, 1152], P('rep', 'dp')
All inputs are finite; a program needn't handle non-finite values.
Results may differ from a plain program's by a relative error of at most 0.018.
Values are sent between devices in bfloat16 or wider.
A program may use at most 2 GiB of HBM per device.

v0:
```python
import jax
import jax.numpy as jnp
from jax import lax

NAMES = ("w_gate", "w_up", "w_down")


def matmul(a, w):
    return jnp.dot(a, w, preferred_element_type=jnp.float32).astype(jnp.bfloat16)


def normed(h):
    wide = h.astype(jnp.float32)
    scale = lax.rsqrt(jnp.mean(wide**2, -1, keepdims=True) + 1e-6)
    return (wide * scale).astype(jnp.bfloat16)


def layer(h, w):
    a = normed(h)
    gate = jnp.dot(a, w["w_gate"], preferred_element_type=jnp.float32)
    up = jnp.dot(a, w["w_up"], preferred_element_type=jnp.float32)
    return h + matmul((jax.nn.silu(gate) * up).astype(jnp.bfloat16), w["w_down"])


def stack(weights, h):
    for number in range(weights["w_gate"].shape[0]):
        h = layer(h, {name: w[number] for name, w in weights.items()})
    return h


def solution(mesh):
    groups = mesh.shape["rep"]

    def step(x, dy, *weights):
        shape = x.shape
        x, dy = (t.reshape(groups, -1, *t.shape[1:]) for t in (x, dy))

        def of_a_group(x, dy):
            _, back = jax.vjp(stack, dict(zip(NAMES, weights, strict=True)), x)
            by_weights, by_x = back(dy)
            return (by_x, *(by_weights[name] for name in NAMES))

        by_x, *by_weights = jax.vmap(of_a_group)(x, dy)
        return (by_x.reshape(shape), *(t.reshape(-1, *t.shape[2:]) for t in by_weights))

    return step
```

profile of v0, /device:TPU:0, one launch (start us, length us, event | category | flops | bytes accessed | tf_op | source)
XLA Modules:
  0.0 1351.4 jit_solution(14501386086963028216)
XLA Ops:
  17.8 6.9 copy.1
  35.3 36.6 %all-gather.30.cloned.1.call-done = bf16[1,1152,4608]{2,1,0:T(8,128)(2,1)} async-done(((bf16[1,144,4608]{2,1,0:T(8,128)(2,1)}), bf16[1,1152,4608]{2,1,0:T(8,128)(2,1)}) %all-gather.30.cloned.1.call-update) | async-done | bytes 10616848 | tf_op jit(solution)/vmap(jvp())/squeeze | solution.py:27
  71.9 31.9 %fusion.48 = f32[2048,4608]{1,0:T(8,128)} fusion(bf16[1,1152,4608]{2,1,0:T(8,128)(2,1)} %all-gather.30.cloned.1.call-done, bf16[1,2048,1152]{1,2,0:T(8,128)(2,1)} %copy.1, f32[2048]{0:T(1024)S(1)} %bitcast.307), kind=kOutput, calls=%fused_computation.69 | convolution fusion | flops 21750349824 | bytes 53092352 | tf_op jit(solution)/vmap(jvp())/dot_general | solution.py:20
  103.8 28.6 %all-gather.32.cloned.1.call-done = bf16[1,1152,4608]{2,1,0:T(8,128)(2,1)} async-done(((bf16[1,144,4608]{2,1,0:T(8,128)(2,1)}), bf16[1,1152,4608]{2,1,0:T(8,128)(2,1)}) %all-gather.32.cloned.1.call-update) | async-done | bytes 10616848 | tf_op jit(solution)/vmap(jvp())/squeeze | solution.py:27
  132.4 31.9 %fusion.44 = f32[2048,4608]{1,0:T(8,128)} fusion(bf16[1,1152,4608]{2,1,0:T(8,128)(2,1)} %all-gather.32.cloned.1.call-done, bf16[1,2048,1152]{1,2,0:T(8,128)(2,1)} %copy.1, f32[2048]{0:T(1024)S(1)} %bitcast.308), kind=kOutput, calls=%fused_computation.65 | convolution fusion | flops 21750349824 | bytes 53092352 | tf_op jit(solution)/vmap(jvp())/dot_general | solution.py:21
  164.3 33.0 %fusion.24 = bf16[2048,4608]{1,0:T(8,128)(2,1)} fusion(f32[2048,4608]{1,0:T(8,128)} %fusion.44, f32[2048,4608]{1,0:T(8,128)} %fusion.48), kind=kLoop, calls=%fused_computation.36 | loop fusion | flops 56623104 | bytes 94371840
  197.3 31.8 %fusion.57 = (f32[2048]{0:T(1024)S(1)}, bf16[1,2048,1152]{1,2,0:T(8,128)(2,1)}) fusion(bf16[1,2048,1152]{1,2,0:T(8,128)(2,1)} %copy.1, bf16[2048,4608]{1,0:T(8,128)(2,1)} %fusion.24, bf16[1,4608,1152]{2,1,0:T(8,128)(2,1)} %all-gather.34.cloned.1.call-done), kind=kOutput, calls=%fused_computation.78 | convolution fusion | flops 21755066368 | bytes 38936576 | tf_op jit(solution)/vmap(jvp())/dot_general | solution.py:9
  229.7 23.1 %all-gather.40.cloned.1.call-done = bf16[1,1152,4608]{2,1,0:T(8,128)(2,1)} async-done(((bf16[1,144,4608]{2,1,0:T(8,128)(2,1)}), bf16[1,1152,4608]{2,1,0:T(8,128)(2,1)}) %all-gather.40.cloned.1.call-update) | async-done | bytes 10616848 | tf_op jit(solution)/vmap(jvp())/squeeze | solution.py:27
  252.8 31.8 %fusion.32 = f32[2048,4608]{1,0:T(8,128)} fusion(bf16[1,1152,4608]{2,1,0:T(8,128)(2,1)} %all-gather.40.cloned.1.call-done, bf16[1,2048,1152]{1,2,0:T(8,128)(2,1)} %get-tuple-element.11, f32[2048]{0:T(1024)S(1)} %bitcast.312), kind=kOutput, calls=%fused_computation.53 | convolution fusion | flops 21750349824 | bytes 53092352 | tf_op jit(solution)/vmap(jvp())/dot_general | solution.py:21
  284.6 28.6 %all-gather.36.cloned.1.call-done = bf16[1,1152,4608]{2,1,0:T(8,128)(2,1)} async-done(((bf16[1,144,4608]{2,1,0:T(8,128)(2,1)}), bf16[1,1152,4608]{2,1,0:T(8,128)(2,1)}) %all-gather.36.cloned.1.call-update) | async-done | bytes 10616848 | tf_op jit(solution)/vmap(jvp())/squeeze | solution.py:27
  313.2 32.0 %fusion.38 = f32[2048,4608]{1,0:T(8,128)} fusion(bf16[1,1152,4608]{2,1,0:T(8,128)(2,1)} %all-gather.36.cloned.1.call-done, bf16[1,2048,1152]{1,2,0:T(8,128)(2,1)} %get-tuple-element.11, f32[2048]{0:T(1024)S(1)} %bitcast.313), kind=kOutput, calls=%fused_computation.59 | convolution fusion | flops 21750349824 | bytes 53092352 | tf_op jit(solution)/vmap(jvp())/dot_general | solution.py:20
  345.2 27.8 %all-gather.38.cloned.1.call-done = bf16[1,4608,1152]{2,1,0:T(8,128)(2,1)} async-done(((bf16[1,576,1152]{2,1,0:T(8,128)(2,1)}), bf16[1,4608,1152]{2,1,0:T(8,128)(2,1)}) %all-gather.38.cloned.1.call-update) | async-done | bytes 10616848 | tf_op jit(solution)/vmap(jvp())/squeeze | solution.py:27
  373.0 31.4 %convolution_convert_fusion.1 = bf16[2048,4608]{1,0:T(8,128)(2,1)} fusion(bf16[1,4608,1152]{2,1,0:T(8,128)(2,1)} %all-gather.38.cloned.1.call-done, bf16[1,2048,1152]{2,1,0:T(8,128)(2,1)} %param), kind=kOutput, calls=%fused_computation.35 | convolution fusion | flops 21752709120 | bytes 34209792 | tf_op jit(solution)/vmap(transpose(jvp()))/dot_general | solution.py:9
  404.4 30.6 %fusion.4 = bf16[2048,4608]{1,0:T(8,128)(2,1)S(1)} fusion(f32[2048,4608]{1,0:T(8,128)} %fusion.38, f32[2048,4608]{1,0:T(8,128)} %fusion.32, bf16[2048,4608]{1,0:T(8,128)(2,1)} %convolution_convert_fusion.1), kind=kLoop, calls=%fused_computation.10 | loop fusion | flops 113246208 | bytes 113246208
  441.5 25.5 %fusion.66 = bf16[2048,1152]{0,1:T(8,128)(2,1)} fusion(bf16[2048,4608]{1,0:T(8,128)(2,1)S(1)} %fusion.4, bf16[1,1152,4608]{2,1,0:T(8,128)(2,1)} %all-gather.36.cloned.1.call-done), kind=kOutput, calls=%fused_computation.83 | convolution fusion | flops 21743271936 | bytes 34209792 | tf_op jit(solution)/vmap(transpose(jvp()))/dot_general | solution.py:20
  467.0 38.5 %fusion.59 = (f32[2048]{0:T(1024)S(1)}, bf16[1,2048,1152]{1,2,0:T(8,128)(2,1)}) fusion(bf16[1,2048,1152]{1,2,0:T(8,128)(2,1)} %get-tuple-element.11, bf16[2048,1152]{0,1:T(8,128)(2,1)} %fusion.66, bf16[1,1152,4608]{2,1,0:T(8,128)(2,1)} %all-gather.40.cloned.1.call-done, bf16[2048,4608]{1,0:T(8,128)(2,1)} %convolution_convert_fusion.1, f32[2048,4608]{1,0:T(8,128)} %fusion.38), kind=kOutput, calls=%fused_computation.80 | convolution fusion | flops 21814048768 | bytes 81403904 | tf_op jit(solution)/vmap(transpose(jvp()))/dot_general | solution.py:21
  505.5 8.6 fusion.108
  516.4 31.1 %fusion.109 = f32[1152,4608]{0,1:T(8,128)} fusion(bf16[2048,4608]{1,0:T(8,128)(2,1)} %fusion.24, bf16[1,2048,1152]{1,2,0:T(8,128)(2,1)S(1)} %fusion.108), kind=kOutput, calls=%fused_computation.96 | convolution fusion | flops 21743271936 | bytes 44826624 | tf_op jit(solution)/vmap(transpose(jvp()))/dot_general | solution.py:9
  547.5 48.8 %fusion.26 = f32[4608,1152]{1,0:T(8,128)} fusion(f32[2048,4608]{1,0:T(8,128)} %fusion.32, f32[2048,4608]{1,0:T(8,128)} %fusion.38, bf16[1,2048,1152]{2,1,0:T(8,128)(2,1)} %param), kind=kOutput, calls=%fused_computation.38 | convolution fusion | flops 21799895040 | bytes 101449728 | tf_op jit(solution)/vmap(transpose(jvp()))/dot_general | solution.py:9
  597.1 36.5 %fusion.20 = f32[4608,1152]{0,1:T(8,128)} fusion(bf16[2048,4608]{1,0:T(8,128)(2,1)} %convolution_convert_fusion.1, f32[2048,4608]{1,0:T(8,128)} %fusion.38, bf16[1,2048,1152]{1,2,0:T(8,128)(2,1)} %get-tuple-element.11, f32[2048]{0:T(1024)S(1)} %bitcast.315), kind=kOutput, calls=%fused_computation.32 | convolution fusion | flops 21806972928 | bytes 82583552 | tf_op jit(solution)/vmap(transpose(jvp()))/dot_general | solution.py:21
  633.7 31.7 %convolution_convert_fusion = bf16[2048,4608]{1,0:T(8,128)(2,1)} fusion(bf16[1,4608,1152]{2,1,0:T(8,128)(2,1)} %all-gather.34.cloned.1.call-done, bf16[1,2048,1152]{1,2,0:T(8,128)(2,1)} %copy-done.2), kind=kOutput, calls=%fused_computation.34 | convolution fusion | flops 21752709120 | bytes 34209792 | tf_op jit(solution)/vmap(transpose(jvp()))/dot_general | solution.py:9
  665.4 40.6 %fusion.16 = f32[4608,1152]{0,1:T(8,128)} fusion(bf16[2048,4608]{1,0:T(8,128)(2,1)} %convolution_convert_fusion, f32[2048,4608]{1,0:T(8,128)} %fusion.48, bf16[1,2048,1152]{1,2,0:T(8,128)(2,1)} %copy.1, f32[2048]{0:T(1024)S(1)} %bitcast.309), kind=kOutput, calls=%fused_computation.30 | convolution fusion | flops 21806972928 | bytes 82583552 | tf_op jit(solution)/vmap(transpose(jvp()))/dot_general | solution.py:21
  706.7 28.7 %fusion.120 = f32[4608,1152]{0,1:T(8,128)} fusion(bf16[2048,4608]{1,0:T(8,128)(2,1)} %copy-done, bf16[1,2048,1152]{1,2,0:T(8,128)(2,1)} %get-tuple-element.11, f32[2048]{0:T(1024)S(1)} %bitcast.316), kind=kOutput, calls=%fused_computation.102 | convolution fusion | flops 21750349824 | bytes 44834816 | tf_op jit(solution)/vmap(transpose(jvp()))/dot_general | solution.py:20
  735.5 33.2 %fusion.7 = bf16[2048,4608]{1,0:T(8,128)(2,1)S(1)} fusion(f32[2048,4608]{1,0:T(8,128)} %fusion.48, f32[2048,4608]{1,0:T(8,128)} %fusion.44, bf16[2048,4608]{1,0:T(8,128)(2,1)} %convolution_convert_fusion), kind=kLoop, calls=%fused_computation.13 | loop fusion | flops 113246208 | bytes 113246208
  775.2 26.3 %fusion.115 = f32[4608,1152]{0,1:T(8,128)} fusion(bf16[2048,4608]{1,0:T(8,128)(2,1)S(1)} %fusion.7, bf16[1,2048,1152]{1,2,0:T(8,128)(2,1)} %copy.1, f32[2048]{0:T(1024)S(1)} %bitcast.310), kind=kOutput, calls=%fused_computation.101 | convolution fusion | flops 21750349824 | bytes 44834816 | tf_op jit(solution)/vmap(transpose(jvp()))/dot_general | solution.py:20
  801.5 29.6 %fusion.60 = bf16[2048,1152]{0,1:T(8,128)(2,1)} fusion(bf16[2048,4608]{1,0:T(8,128)(2,1)} %copy-done.1, bf16[1,1152,4608]{2,1,0:T(8,128)(2,1)} %all-gather.30.cloned.1.call-done), kind=kOutput, calls=%fused_computation.81 | convolution fusion | flops 21743271936 | bytes 34209792 | tf_op jit(solution)/vmap(transpose(jvp()))/dot_general | solution.py:20
  831.2 43.5 %fusion.56 = (f32[2048]{0:T(1024)S(1)}, bf16[1,2048,1152]{1,2,0:T(8,128)(2,1)}) fusion(bf16[1,2048,1152]{1,2,0:T(8,128)(2,1)} %copy.1, bf16[2048,1152]{0,1:T(8,128)(2,1)} %fusion.60, bf16[1,1152,4608]{2,1,0:T(8,128)(2,1)} %all-gather.32.cloned.1.call-done, bf16[2048,4608]{1,0:T(8,128)(2,1)} %convolution_convert_fusion, f32[2048,4608]{1,0:T(8,128)} %fusion.48), kind=kOutput, calls=%fused_computation.77 | convolution fusion | flops 21814048768 | bytes 81403904 | tf_op jit(solution)/vmap(transpose(jvp()))/dot_general | solution.py:21
  874.7 11.7 fusion.107
  899.0 43.6 %reduce-scatter.23.cloned.1.call-done = f32[4608,144]{0,1:T(8,128)} async-done(((f32[4608,1152]{0,1:T(8,128)}), f32[4608,144]{0,1:T(8,128)}) %reduce-scatter.23.cloned.1.call-update) | async-done | bytes 2654224
  944.4 130.8 %reduce-scatter.25.cloned.1.call-done = f32[4608,144]{0,1:T(8,128)} async-done(((f32[4608,1152]{0,1:T(8,128)}), f32[4608,144]{0,1:T(8,128)}) %reduce-scatter.25.cloned.1.call-update) | async-done | bytes 2654224
  1078.8 129.3 %reduce-scatter.19.cloned.1.call-done = f32[4608,144]{0,1:T(8,128)} async-done(((f32[4608,1152]{0,1:T(8,128)}), f32[4608,144]{0,1:T(8,128)}) %reduce-scatter.19.cloned.1.call-update) | async-done | bytes 2654224
  1210.0 130.8 %reduce-scatter.21.cloned.1.call-done = f32[4608,144]{0,1:T(8,128)} async-done(((f32[4608,1152]{0,1:T(8,128)}), f32[4608,144]{0,1:T(8,128)}) %reduce-scatter.21.cloned.1.call-update) | async-done | bytes 2654224
  (76 shorter events, 62.0 us)
Async XLA Ops:
  7.2 7.1 copy-start.3
  7.2 64.7 %all-gather.30.cloned.1.call-start = ((), (), s32[]{:S(2)}) async-start(), calls=%async_computation.6 | async-start | bytes 11943936 | tf_op jit(solution)/vmap(jvp())/squeeze | solution.py:27
  10.8 121.6 %all-gather.32.cloned.1.call-start = ((), (), s32[]{:S(2)}) async-start(), calls=%async_computation.7 | async-start | bytes 11943936 | tf_op jit(solution)/vmap(jvp())/squeeze | solution.py:27
  14.3 183.0 %all-gather.34.cloned.1.call-start = ((), (), s32[]{:S(2)}) async-start(), calls=%async_computation.8 | async-start | bytes 11943936 | tf_op jit(solution)/vmap(jvp())/squeeze | solution.py:27
  16.0 236.7 %all-gather.40.cloned.1.call-start = ((), (), s32[]{:S(2)}) async-start(), calls=%async_computation.11 | async-start | bytes 11943936 | tf_op jit(solution)/vmap(jvp())/squeeze | solution.py:27
  16.6 296.6 %all-gather.36.cloned.1.call-start = ((), (), s32[]{:S(2)}) async-start(), calls=%async_computation.9 | async-start | bytes 11943936 | tf_op jit(solution)/vmap(jvp())/squeeze | solution.py:27
  17.2 355.8 %all-gather.38.cloned.1.call-start = ((), (), s32[]{:S(2)}) async-start(), calls=%async_computation.10 | async-start | bytes 11943936 | tf_op jit(solution)/vmap(jvp())/squeeze | solution.py:27
  17.8 875.4 %reduce-scatter.29.cloned.1.call-start = ((), (), s32[]{:S(2)}) async-start(), calls=%async_computation.17 | async-start | bytes 23887872
  28.1 0.6 copy-start.4
  28.7 103.7 %copy-start.8 = (f32[1,2048]{1,0:T(1,128)}, f32[1,2048]{1,0:T(1,128)S(1)}, u32[]{:S(2)}) copy-start(f32[1,2048]{1,0:T(1,128)S(1)} %rsqrt.22) | copy-start | bytes 24580
  229.1 0.6 copy-start.6
  229.7 83.5 %copy-start.10 = (f32[1,2048]{1,0:T(1,128)}, f32[1,2048]{1,0:T(1,128)S(1)}, u32[]{:S(2)}) copy-start(f32[1,2048]{1,0:T(1,128)S(1)} %rsqrt.23) | copy-start | bytes 24580
  435.0 6.5 copy-start
  467.0 38.5 %copy-start.7 = (f32[2048]{0:T(1024)S(1)}, f32[2048]{0:T(1024)}, u32[]{:S(2)}) copy-start(f32[2048]{0:T(1024)} %copy-done.6) | copy-start | bytes 24580
  467.0 38.5 %copy-start.11 = (f32[1,2048]{1,0:T(1,128)S(1)}, f32[1,2048]{1,0:T(1,128)}, u32[]{:S(2)}) copy-start(f32[1,2048]{1,0:T(1,128)} %copy-done.10) | copy-start | bytes 24580
  514.2 2.2 copy-start.2
  547.5 347.9 %reduce-scatter.27.cloned.1.call-start = ((), (), s32[]{:S(2)}) async-start(), calls=%async_computation.16 | async-start | bytes 23887872
  596.4 0.7 copy-start.12
  596.4 346.2 %reduce-scatter.23.cloned.1.call-start = ((), (), s32[]{:S(2)}) async-start(), calls=%async_computation.14 | async-start | bytes 23887872
  633.6 31.8 %copy-start.9 = (f32[1,2048]{1,0:T(1,128)S(1)}, f32[1,2048]{1,0:T(1,128)}, u32[]{:S(2)}) copy-start(f32[1,2048]{1,0:T(1,128)} %copy-done.8) | copy-start | bytes 24580
  633.6 441.6 %reduce-scatter.25.cloned.1.call-start = ((), (), s32[]{:S(2)}) async-start(), calls=%async_computation.15 | async-start | bytes 23887872
  706.0 0.7 copy-start.13
  706.0 502.0 %reduce-scatter.19.cloned.1.call-start = ((), (), s32[]{:S(2)}) async-start(), calls=%async_computation.12 | async-start | bytes 23887872
  735.4 605.4 %reduce-scatter.21.cloned.1.call-start = ((), (), s32[]{:S(2)}) async-start(), calls=%async_computation.13 | async-start | bytes 23887872
  768.7 6.5 copy-start.1
  831.2 43.5 %copy-start.5 = (f32[2048]{0:T(1024)S(1)}, f32[2048]{0:T(1024)}, u32[]{:S(2)}) copy-start(f32[2048]{0:T(1024)} %copy-done.4) | copy-start | bytes 24580
Sparse Core Ops, SparseCore 0:
  10.9 60.9 all-gather.29
  74.2 58.1 all-gather.31
  134.2 58.1 all-gather.33
  194.6 58.1 all-gather.39
  255.0 58.1 all-gather.35
  314.8 58.1 all-gather.37
  547.6 129.2 reduce-scatter.28
  680.4 129.2 reduce-scatter.26
  813.3 129.2 reduce-scatter.22
  945.9 129.2 reduce-scatter.24
  1078.8 129.2 reduce-scatter.18
  1211.5 129.2 reduce-scatter.20
where the time goes:
time: 1360 us; the launch traced here: 1350 us
  waiting for transfers between devices  581 us (43%)
  matrix products  572 us (42%)
  other arithmetic  137 us (10%)
  local copies, waits for them, and re-layouts  46.6 us (3%)
  between operations  14.6 us (1%)
    unnamed x18, waiting for transfers between devices  436 us
    dot_general x6, matrix products, layer(): up = jnp.dot(a, w['w_up'], preferred_element_type=jnp.float32)  223 us
    dot_general x5, matrix products, matmul(): jnp.dot(a, w, preferred_element_type=jnp.float32).astype(jnp.bfloat16)  175 us
    dot_general x6, matrix products, layer(): gate = jnp.dot(a, w['w_gate'], preferred_element_type=jnp.float32)  174 us
    squeeze x6, waiting for transfers between devices, stack(): h = layer(h, {name: w[number] for name, w in weights.items()})  145 us
    unnamed x3, other arithmetic  96.8 us
    unnamed x31, local copies, waits for them, and re-layouts  37.9 us
  transfers between devices with their start and end apart: 12, of which 9 were waited for; matrix products, arithmetic and copies ran while one was open for 42% of the time, Pallas kernels for 0%

commit v1 on v0

v1 whole, which is shorter than its diff:
```python
import functools

import jax
import jax.numpy as jnp
from jax import lax
from jax.experimental import pallas as pl
from jax.experimental.pallas import tpu as pltpu
from jax.sharding import PartitionSpec as P


T, D, FF = 2048, 1152, 4608
HALF = FF // 2
RD = D // 8
RF = FF // 8
BF, F32 = jnp.bfloat16, jnp.float32
VMEM_LIMIT = 60 * 1024 * 1024
NT = (((1,), (1,)), ((), ()))
TN = (((0,), (0,)), ((), ()))
ANY = pl.BlockSpec(memory_space=pl.ANY)


def first(i):
    return i ^ (4 if i % 2 == 0 else 2)


def second(i):
    return i ^ (2 if i % 2 == 0 else 4)


def partner(i):
    return i ^ 1


def send(v, to):
    return lax.ppermute(v, "dp", [(i, to(i)) for i in range(8)])


def dot(a, b, dims=None):
    if dims is None:
        return jnp.dot(a, b, preferred_element_type=F32)
    return lax.dot_general(a, b, dims, preferred_element_type=F32)


def params(**kw):
    return pltpu.CompilerParams(vmem_limit_bytes=VMEM_LIMIT, **kw)


def cost(flops, nbytes):
    return pl.CostEstimate(flops=flops, bytes_accessed=nbytes, transcendentals=0)


def places():
    me = lax.axis_index("dp")
    core = me % 2
    one, two = 4 - 2 * core, 2 + 2 * core
    other = me ^ 1
    where = [me, me ^ one, me ^ two, me ^ 6, other, other ^ two, other ^ one, other ^ 6]
    slots = []
    for b in range(8):
        chips = (b ^ me) // 2
        ahead = 2 if b % 2 == 0 else 1
        slot = jnp.where(chips == 0, 0, jnp.where(chips == 3, 1, jnp.where(chips == ahead, 2, 3)))
        slots.append(slot + 4 * ((b ^ me) % 2))
    return jnp.stack([v.astype(jnp.int32) for v in (*where, *slots)])


GU_M, GU_N, GU_C = 512, 768, 128
GU_STEPS = HALF // GU_N


def gu_body(pos, a_ref, *refs):
    blocks, (act_ref, s_ref, t_ref, wg, wu, sem) = refs[:8], refs[8:]
    n, m = pl.program_id(0), pl.program_id(1)

    def copies(k):
        cols = pl.ds(k * GU_N, GU_N)
        out = []
        for j, block in enumerate(blocks):
            rows = pl.ds(pl.multiple_of(pos[j] * RD, 16), RD)
            out.append(pltpu.make_async_copy(block.at[pl.ds(0, RD), cols], wg.at[k, rows, :], sem.at[k, 2 * j]))
            out.append(pltpu.make_async_copy(block.at[pl.ds(RD, RD), cols], wu.at[k, rows, :], sem.at[k, 2 * j + 1]))
        return out

    @pl.when((n == 0) & (m == 0))
    def _():
        for k in range(GU_STEPS):
            for c in copies(k):
                c.start()

    for k in range(GU_STEPS):

        @pl.when((n == k) & (m == 0))
        def _():
            for c in copies(k):
                c.wait()

    for c in range(0, GU_M, GU_C):
        r = slice(c, c + GU_C)
        a = a_ref[r, :]
        g = dot(a, wg[n])
        u = dot(a, wu[n])
        sig = jax.nn.sigmoid(g)
        s = g * sig
        s_ref[r, :] = s
        t_ref[r, :] = u * (sig + s * (1 - sig))
        act_ref[r, :] = (s * u).astype(BF)


def gate_up(pos, a, blocks):
    out = pl.BlockSpec((GU_M, GU_N), lambda n, m, pos: (m, n))
    return pl.pallas_call(
        gu_body,
        grid_spec=pltpu.PrefetchScalarGridSpec(
            num_scalar_prefetch=1,
            grid=(GU_STEPS, T // GU_M),
            in_specs=[pl.BlockSpec((GU_M, D), lambda n, m, pos: (m, 0))] + [ANY] * 8,
            out_specs=[out] * 3,
            scratch_shapes=[
                pltpu.VMEM((GU_STEPS, D, GU_N), BF),
                pltpu.VMEM((GU_STEPS, D, GU_N), BF),
                pltpu.SemaphoreType.DMA((GU_STEPS, 16)),
            ],
        ),
        out_shape=[jax.ShapeDtypeStruct((T, HALF), d) for d in (BF, F32, F32)],
        compiler_params=params(),
        cost_estimate=cost(4 * T * D * HALF, 70_000_000),
        name="gate_up",
    )(pos, a, *blocks)


def norm_of(wide):
    return lax.rsqrt(jnp.mean(wide * wide, -1, keepdims=True) + 1e-6)


def normed(h, a_ref, at_ref):
    wide = h.astype(F32)
    a = (wide * norm_of(wide)).astype(BF)
    a_ref[...] = a
    at_ref[...] = a.astype(F32).T.astype(BF)


def norm_body(h_ref, a_ref, at_ref):
    normed(h_ref[...], a_ref, at_ref)


def norm(h):
    row = pl.BlockSpec((DN_M, D), lambda m: (m, 0))
    return pl.pallas_call(
        norm_body,
        grid=(T // DN_M,),
        in_specs=[row],
        out_specs=[row, pl.BlockSpec((D, DN_M), lambda m: (0, m))],
        out_shape=[jax.ShapeDtypeStruct((T, D), BF), jax.ShapeDtypeStruct((D, T), BF)],
        compiler_params=params(),
        cost_estimate=cost(1_000_000_000, 14_000_000),
        name="norm",
    )(h)


DN_M = 512


def down_body(pos, aa, ab, h_ref, *refs):
    blocks, (h1_ref, a1_ref, at_ref, wd, sem) = refs[:8], refs[8:]

    @pl.when(pl.program_id(0) == 0)
    def _():
        cs = [
            pltpu.make_async_copy(b, wd.at[pl.ds(pl.multiple_of(pos[j] * RF, 16), RF), :], sem.at[j])
            for j, b in enumerate(blocks)
        ]
        for c in cs:
            c.start()
        for c in cs:
            c.wait()

    out = dot(aa[...], wd[:HALF]) + dot(ab[...], wd[HALF:])
    h1 = (h_ref[...].astype(F32) + out.astype(BF).astype(F32)).astype(BF)
    h1_ref[...] = h1
    normed(h1, a1_ref, at_ref)


def down(pos, aa, ab, h, blocks):
    row = lambda n: pl.BlockSpec((DN_M, n), lambda m, pos: (m, 0))
    return pl.pallas_call(
        down_body,
        grid_spec=pltpu.PrefetchScalarGridSpec(
            num_scalar_prefetch=1,
            grid=(T // DN_M,),
            in_specs=[row(HALF), row(HALF), row(D)] + [ANY] * 8,
            out_specs=[row(D), row(D), pl.BlockSpec((D, DN_M), lambda m, pos: (0, m))],
            scratch_shapes=[pltpu.VMEM((FF, D), BF), pltpu.SemaphoreType.DMA((8,))],
        ),
        out_shape=[jax.ShapeDtypeStruct((T, D), BF)] * 2 + [jax.ShapeDtypeStruct((D, T), BF)],
        compiler_params=params(),
        cost_estimate=cost(2 * T * D * FF, 45_000_000),
        name="down",
    )(pos, aa, ab, h, *blocks)


def by_down_body(aa, ab, dh_ref, out_ref):
    c = pl.program_id(0)

    @pl.when(c < 2)
    def _():
        out_ref[...] = dot(aa[...], dh_ref[...], TN).astype(BF)

    @pl.when(c >= 2)
    def _():
        out_ref[...] = dot(ab[...], dh_ref[...], TN).astype(BF)


def by_down(aa, ab, dh):
    return pl.pallas_call(
        by_down_body,
        grid=(4,),
        in_specs=[
            pl.BlockSpec((T, D), lambda c: (0, jnp.minimum(c, 1))),
            pl.BlockSpec((T, D), lambda c: (0, jnp.maximum(c - 2, 0))),
            pl.BlockSpec((T, D), lambda c: (0, 0)),
        ],
        out_specs=pl.BlockSpec((D, D), lambda c: (c, 0)),
        out_shape=jax.ShapeDtypeStruct((FF, D), BF),
        compiler_params=params(),
        cost_estimate=cost(2 * T * D * FF, 35_000_000),
        name="by_down",
    )(aa, ab, dh)


BG_N, BG_C = 256, 512


def by_gate_up_body(half, slots, pos, dh_ref, s_ref, t_ref, at_ref, *refs):
    blocks, (dg_ref, du_ref, out, wd, sem) = refs[:8], refs[8:]
    n = pl.program_id(0)

    def each(what):
        for j, b in enumerate(blocks):

            @pl.when(pos[j] // 4 == half)
            def _():
                rows = pl.ds(pl.multiple_of((pos[j] % 4) * RF, 16), RF)
                what(pltpu.make_async_copy(b, wd.at[rows, :], sem.at[j]))

    @pl.when(n == 0)
    def _():
        each(lambda c: c.start())
        each(lambda c: c.wait())

    w = wd[pl.ds(pl.multiple_of(n * BG_N, BG_N), BG_N), :]
    for c in range(0, T, BG_C):
        r = slice(c, c + BG_C)
        d = dot(dh_ref[r, :], w, NT).astype(BF).astype(F32)
        dg_ref[r, :] = (d * t_ref[r, :]).astype(BF)
        du_ref[r, :] = (d * s_ref[r, :]).astype(BF)
    for k, v in enumerate((dg_ref, du_ref)):
        res = dot(at_ref[...], v[...]).astype(BF)
        for b in range(8):
            out[pos[8 + b] if slots else b, k * RD : (k + 1) * RD, :] = res[b * RD : (b + 1) * RD]


def by_gate_up(pos, half, slots, dh, s, t, at, blocks):
    full = lambda shape: pl.BlockSpec(shape, lambda n, pos: (0,) * len(shape), pipeline_mode=pl.Buffered(1))
    col = pl.BlockSpec((T, BG_N), lambda n, pos: (0, n))
    grad = pl.BlockSpec((8, 2 * RD, BG_N), lambda n, pos: (0, 0, n))
    return pl.pallas_call(
        functools.partial(by_gate_up_body, half, slots),
        grid_spec=pltpu.PrefetchScalarGridSpec(
            num_scalar_prefetch=1,
            grid=(HALF // BG_N,),
            in_specs=[full((T, D)), col, col, full((D, T))] + [ANY] * 8,
            out_specs=[col, col, grad],
            scratch_shapes=[pltpu.VMEM((HALF, D), BF), pltpu.SemaphoreType.DMA((8,))],
        ),
        out_shape=[jax.ShapeDtypeStruct((T, HALF), BF)] * 2 + [jax.ShapeDtypeStruct((8, 2 * RD, HALF), BF)],
        compiler_params=params(),
        cost_estimate=cost(6 * T * D * HALF, 85_000_000),
    )(pos, dh, s, t, at, *blocks)


DA_M = 512


def by_a_body(part, pos, ga, gb, *refs):
    extra, blocks, (out_ref, wa, wb, sem) = refs[:-20], refs[-20:-4], refs[-4:]
    first_step = pl.program_id(0) == 0

    def copies(k, w):
        return [
            pltpu.make_async_copy(
                blocks[8 * k + j].at[pl.ds(part * RD, RD), :],
                w.at[pl.ds(pl.multiple_of(pos[j] * RD, 16), RD), :],
                sem.at[k, j],
            )
            for j in range(8)
        ]

    @pl.when(first_step)
    def _():
        for c in copies(0, wa) + copies(1, wb):
            c.start()
        for c in copies(0, wa):
            c.wait()

    da = dot(ga[...], wa[...], NT)

    @pl.when(first_step)
    def _():
        for c in copies(1, wb):
            c.wait()

    da = (da + dot(gb[...], wb[...], NT)).astype(BF)
    if not extra:
        out_ref[...] = da
        return
    before, h_ref, dh_ref = extra
    da = (da.astype(F32) + before[...].astype(F32)).astype(BF).astype(F32)
    wide = h_ref[...].astype(F32)
    scale = norm_of(wide)
    along = jnp.mean(da * wide, -1, keepdims=True)
    by_h = (scale * da - wide * (scale * scale * scale * along)).astype(BF)
    out_ref[...] = (dh_ref[...].astype(F32) + by_h.astype(F32)).astype(BF)


def by_a(pos, part, ga, gb, blocks_a, blocks_b, extra=()):
    row = lambda n: pl.BlockSpec((DA_M, n), lambda m, pos: (m, 0))
    return pl.pallas_call(
        functools.partial(by_a_body, part),
        grid_spec=pltpu.PrefetchScalarGridSpec(
            num_scalar_prefetch=1,
            grid=(T // DA_M,),
            in_specs=[row(HALF), row(HALF)] + [row(D)] * len(extra) + [ANY] * 16,
            out_specs=row(D),
            scratch_shapes=[pltpu.VMEM((D, HALF), BF), pltpu.VMEM((D, HALF), BF), pltpu.SemaphoreType.DMA((2, 8))],
        ),
        out_shape=jax.ShapeDtypeStruct((T, D), BF),
        compiler_params=params(),
        cost_estimate=cost(2 * T * D * FF, 45_000_000),
    )(pos, ga, gb, *extra, *blocks_a, *blocks_b)


def after(v, *others):
    return lax.optimization_barrier((v, *others))[0]


def gather_ahead(v):
    return send(v, first), send(v, second)


def gather_rest(v, one, two):
    across = send(one, second)
    near = [send(b, partner) for b in (v, one, two)]
    return [v, one, two, across, *near, send(across, partner)]


def by_hand(terms):
    own, part = terms[:4], terms[4:]
    got = send(part, partner)
    pair = lambda k: own[k].astype(F32) + got[k].astype(F32)
    across = send(pair(1).astype(BF), first)
    one = send(pair(2).astype(BF), first)
    two = send((pair(3) + across.astype(F32)).astype(BF), second)
    return (pair(0) + one.astype(F32) + two.astype(F32)).astype(BF)


def scatter(terms):
    return lax.psum_scatter(terms.reshape(-1, terms.shape[-1]), "dp", scatter_dimension=0, tiled=True)


def solution(mesh):
    def whole_step(x, dy, w_gate, w_up, w_down):
        x, dy = x[0], dy[0]
        pos = places()
        units = []
        for layer in range(2):
            for half in range(2):
                cols = slice(half * HALF, (half + 1) * HALF)
                units.append(jnp.concatenate([w_gate[layer][:, cols], w_up[layer][:, cols]], 0))
            units.append(w_down[layer])
        ahead, whole = [], []
        for k, v in enumerate(units):
            if k >= 2:
                v = after(v, *ahead[k - (1 if k == 5 else 2)])
            ahead.append(gather_ahead(v))
            units[k] = v
        for v, (one, two) in zip(units, ahead):
            whole.append(gather_rest(v, one, two))
        g0a, g0b, d0, g1a, g1b, d1 = whole

        a0, at0 = norm(x)
        act0a, s0a, t0a = gate_up(pos, a0, g0a)
        act0b, s0b, t0b = gate_up(pos, after(a0, act0a), g0b)
        h1, a1, at1 = down(pos, act0a, act0b, x, d0)
        act1a, s1a, t1a = gate_up(pos, a1, g1a)
        act1b, s1b, t1b = gate_up(pos, after(a1, act1a), g1b)

        def backward(i, dh, h, at, acts, s, t, ga, gb, d):
            by_d = by_down(*acts, dh)
            later = after(dh, by_d)
            dga, dua, by_ga = by_gate_up(pos, 0, False, later, s[0], t[0], at, d)
            later = after(later, by_ga)
            dgb, dub, by_gb = by_gate_up(pos, 1, i == 0, later, s[1], t[1], at, d)
            da = by_a(pos, 0, dga, dgb, ga, gb)
            dh = by_a(pos, 1, dua, dub, ga, gb, (da, h, dh))
            return dh, (scatter(by_d), scatter(by_ga), scatter(by_gb) if i else by_hand(by_gb))

        dh, (gd1, gg1a, gg1b) = backward(1, dy, h1, at1, (act1a, act1b), (s1a, s1b), (t1a, t1b), g1a, g1b, d1)
        dx, (gd0, gg0a, gg0b) = backward(0, dh, x, at0, (act0a, act0b), (s0a, s0b), (t0a, t0b), g0a, g0b, d0)
        by_gate = jnp.stack([jnp.concatenate([p[:RD], q[:RD]], 1) for p, q in ((gg0a, gg0b), (gg1a, gg1b))])
        by_up = jnp.stack([jnp.concatenate([p[RD:], q[RD:]], 1) for p, q in ((gg0a, gg0b), (gg1a, gg1b))])
        return dx[None], by_gate, by_up, jnp.stack([gd0, gd1])

    tokens, rows = P(("rep", "dp"), None, None), P(None, "dp", None)
    return jax.shard_map(
        whole_step,
        mesh=mesh,
        in_specs=(tokens, tokens, rows, rows, rows),
        out_specs=(tokens, *(P("rep", "dp", None),) * 3),
        check_vma=False,
    )
```

time: 1360 us -> 973 us (0.72)
  Pallas kernels: 0 us -> 597 us
  matrix products: 572 us -> 0 us
  waiting for transfers between devices: 581 us -> 288 us
  other arithmetic: 137 us -> 17.7 us
  starting transfers between devices: 0.49 us -> 31.2 us
  local copies, waits for them, and re-layouts: 46.6 us -> 20.4 us
    pallas_call x0 -> x16, Pallas kernels: none -> 597 us  [the longest x4 193 us: by_gate_up(): pl.pallas_call(functools.partial(by_gate_up_body, half, slots), grid_spec...]
    dot_general x17 -> x0, matrix products: 572 us -> none  [the longest x6 223 us: layer(): up = jnp.dot(a, w['w_up'], preferred_element_type=jnp.float32)]
    unnamed x18 -> x5, waiting for transfers between devices: 436 us -> 1.25 us
    ppermute x0 -> x46, waiting for transfers between devices: none -> 184 us  [send(): return lax.ppermute(v, 'dp', [(i, to(i)) for i in range(8)])]
    squeeze x6 -> x0, waiting for transfers between devices: 145 us -> none  [stack(): h = layer(h, {name: w[number] for name, w in weights.items()})]
    reduce_scatter x0 -> x5, waiting for transfers between devices: none -> 103 us  [scatter(): lax.psum_scatter(terms.reshape(-1, terms.shape[-1]), 'dp', scatter_dimens...]
    unnamed x3 -> x0, other arithmetic: 96.8 us -> none
    ppermute x0 -> x46, starting transfers between devices: none -> 31 us  [send(): return lax.ppermute(v, 'dp', [(i, to(i)) for i in range(8)])]
  transfers between devices with their start and end apart: 12 -> 51, of which waited for: 9 -> 15; matrix products, arithmetic and copies ran while one was open for 42% -> 2% of each run, Pallas kernels for 0% -> 62%
where the time goes in v1:
time: 973 us; the launch traced here: 969 us
  Pallas kernels  597 us (61%)
  waiting for transfers between devices  288 us (30%)
  starting transfers between devices  31.2 us (3%)
  local copies, waits for them, and re-layouts  20.4 us (2%)
  other arithmetic  17.7 us (2%)
  between operations  14.5 us (1%)
    pallas_call x4, Pallas kernels, by_gate_up(): pl.pallas_call(functools.partial(by_gate_up_body, half, slots), grid_spec...  193 us
    ppermute x46, waiting for transfers between devices, send(): return lax.ppermute(v, 'dp', [(i, to(i)) for i in range(8)])  184 us
    pallas_call x4, Pallas kernels, by_a(): pl.pallas_call(functools.partial(by_a_body, part), grid_spec=pltpu.Prefet...  155 us
    pallas_call x4, Pallas kernels, gate_up(): pl.pallas_call(gu_body, grid_spec=pltpu.PrefetchScalarGridSpec(num_scalar...  140 us
    reduce_scatter x5, waiting for transfers between devices, scatter(): lax.psum_scatter(terms.reshape(-1, terms.shape[-1]), 'dp', scatter_dimens...  103 us
    pallas_call x2, Pallas kernels, by_down(): pl.pallas_call(by_down_body, grid=(4,), in_specs=[pl.BlockSpec((T, D), la...  64.3 us
    pallas_call x1, Pallas kernels, down(): pl.pallas_call(down_body, grid_spec=pltpu.PrefetchScalarGridSpec(num_scal...  37.3 us
    ppermute x46, starting transfers between devices, send(): return lax.ppermute(v, 'dp', [(i, to(i)) for i in range(8)])  31 us
  transfers between devices with their start and end apart: 51, of which 15 were waited for; matrix products, arithmetic and copies ran while one was open for 2% of the time, Pallas kernels for 62%

profile of v1, /device:TPU:0, one launch (start us, length us, event | category | flops | bytes accessed | tf_op | source)
XLA Modules:
  0.0 969.4 jit_solution(4640215807977831334)
XLA Ops:
  10.4 3.4 collective-permute-start.1
  16.5 26.7 %collective-permute-done.1.refs_2_.refs_5_ = bf16[288,2304]{1,0:T(8,128)(2,1)} collective-permute-done((bf16[288,2304]{1,0:T(8,128)(2,1)S(1)}, bf16[288,2304]{1,0:T(8,128)(2,1)}, u32[]{:S(2)}, u32[]{:S(2)}) %collective-permute-start.1) | collective-permute-done | bytes 1327136 | tf_op jit(solution)/shard_map/ppermute | solution.py:35
  43.2 2.5 collective-permute-start.15
  48.1 27.6 %collective-permute-done.15.refs_2_ = bf16[576,1152]{1,0:T(8,128)(2,1)S(1)} collective-permute-done((bf16[576,1152]{1,0:T(8,128)(2,1)S(1)}, bf16[576,1152]{1,0:T(8,128)(2,1)S(1)}, u32[]{:S(2)}, u32[]{:S(2)}) %collective-permute-start.15) | collective-permute-done | bytes 1327136 | tf_op jit(solution)/shard_map/ppermute | solution.py:35
  79.9 23.8 %collective-permute-done.8.refs_2_.refs_10_.refs_13_ = bf16[288,2304]{1,0:T(8,128)(2,1)} collective-permute-done((bf16[288,2304]{1,0:T(8,128)(2,1)S(1)}, bf16[288,2304]{1,0:T(8,128)(2,1)}, u32[]{:S(2)}, u32[]{:S(2)}) %collective-permute-start.8) | collective-permute-done | bytes 1327136 | tf_op jit(solution)/shard_map/ppermute | solution.py:35
  106.9 23.4 %collective-permute-done.2.refs_3_.refs_6_ = bf16[288,2304]{1,0:T(8,128)(2,1)} collective-permute-done((bf16[288,2304]{1,0:T(8,128)(2,1)}, bf16[288,2304]{1,0:T(8,128)(2,1)}, u32[]{:S(2)}, u32[]{:S(2)}) %collective-permute-start.2) | collective-permute-done | bytes 1327136 | tf_op jit(solution)/shard_map/ppermute | solution.py:35
  130.2 16.1 %collective-permute-done.29.refs_2_.refs_10_.refs_13_ = bf16[288,2304]{1,0:T(8,128)(2,1)S(1)} collective-permute-done((bf16[288,2304]{1,0:T(8,128)(2,1)S(1)}, bf16[288,2304]{1,0:T(8,128)(2,1)S(1)}, u32[]{:S(2)}, u32[]{:S(2)}) %collective-permute-start.29) | collective-permute-done | bytes 1327136 | tf_op jit(solution)/shard_map/ppermute | solution.py:35
  148.5 7.9 norm.1
  163.9 35.1 %gate_up.4 = (bf16[2048,2304]{1,0:T(8,128)(2,1)}, f32[2048,2304]{1,0:T(8,128)}, f32[2048,2304]{1,0:T(8,128)}) custom-call(s32[16]{0:T(128)} %stack.94.pos, bf16[2048,1152]{1,0:T(8,128)(2,1)} %get-tuple-element.45.a_ref, bf16[288,2304]{1,0:T(8,128)(2,1)} %copy-done.5, bf16[288,2304]{1,0:T(8,128)(2,1)} %collective-permute-done.refs_1_.refs_4_, ...), custom_call_target="tpu_custom_call" | custom-call | flops 21743271936 | bytes 70000000 | tf_op jit(solution)/shard_map/gate_up/pallas_call | solution.py:111
  200.4 2.8 collective-permute-done.16.refs_3_
  203.3 34.9 %gate_up.5 = (bf16[2048,2304]{1,0:T(8,128)(2,1)}, f32[2048,2304]{1,0:T(8,128)}, f32[2048,2304]{1,0:T(8,128)}) custom-call(s32[16]{0:T(128)} %stack.94.pos, bf16[2048,1152]{1,0:T(8,128)(2,1)} %get-tuple-element.45.a_ref, bf16[288,2304]{1,0:T(8,128)(2,1)} %copy-done.6, bf16[288,2304]{1,0:T(8,128)(2,1)} %collective-permute-done.7.refs_1_.refs_9_.refs_12_, ...), custom_call_target="tpu_custom_call" | custom-call | flops 21743271936 | bytes 70000000 | tf_op jit(solution)/shard_map/gate_up/pallas_call | solution.py:111
  241.0 37.3 %down.1 = (bf16[2048,1152]{1,0:T(8,128)(2,1)}, bf16[2048,1152]{1,0:T(8,128)(2,1)}, bf16[1152,2048]{1,0:T(8,128)(2,1)}) custom-call(s32[16]{0:T(128)} %stack.94.pos, bf16[2048,2304]{1,0:T(8,128)(2,1)} %get-tuple-element.44.aa, bf16[2048,2304]{1,0:T(8,128)(2,1)} %get-tuple-element.46.ab, bf16[2048,1152]{1,0:T(8,128)(2,1)} %bitcast.62, ...), custom_call_target="tpu_custom_call" | custom-call | flops 21743271936 | bytes 45000000 | tf_op jit(solution)/shard_map/down/pallas_call | solution.py:185
  281.0 35.1 %gate_up.6 = (bf16[2048,2304]{1,0:T(8,128)(2,1)}, f32[2048,2304]{1,0:T(8,128)}, f32[2048,2304]{1,0:T(8,128)}) custom-call(s32[16]{0:T(128)} %stack.94.pos, bf16[2048,1152]{1,0:T(8,128)(2,1)} %get-tuple-element.51.a_ref, bf16[288,2304]{1,0:T(8,128)(2,1)} %copy-done.9, bf16[288,2304]{1,0:T(8,128)(2,1)} %collective-permute-done.21.refs_1_.refs_4_, ...), custom_call_target="tpu_custom_call" | custom-call | flops 21743271936 | bytes 70000000 | tf_op jit(solution)/shard_map/gate_up/pallas_call | solution.py:111
  317.2 34.9 %gate_up.7 = (bf16[2048,2304]{1,0:T(8,128)(2,1)}, f32[2048,2304]{1,0:T(8,128)}, f32[2048,2304]{1,0:T(8,128)}) custom-call(s32[16]{0:T(128)} %stack.94.pos, bf16[2048,1152]{1,0:T(8,128)(2,1)} %get-tuple-element.51.a_ref, bf16[288,2304]{1,0:T(8,128)(2,1)} %copy-done.7, bf16[288,2304]{1,0:T(8,128)(2,1)} %copy-done.17, bf16[288,2304]{1,0:T(8,128)(2,1)} %copy-done.16, ...), custom_call_target="tpu_custom_call" | custom-call | flops 21743271936 | bytes 70000000 | tf_op jit(solution)/shard_map/gate_up/pallas_call | solution.py:111
  352.2 32.1 %by_down.2 = bf16[4608,1152]{1,0:T(8,128)(2,1)} custom-call(bf16[2048,2304]{1,0:T(8,128)(2,1)} %get-tuple-element.50.aa, bf16[2048,2304]{1,0:T(8,128)(2,1)} %get-tuple-element.53.ab, bf16[2048,1152]{1,0:T(8,128)(2,1)} %bitcast.66), custom_call_target="tpu_custom_call" | custom-call | flops 21743271936 | bytes 35000000 | tf_op jit(solution)/shard_map/by_down/pallas_call | solution.py:214
  388.1 15.2 %collective-permute-done.36.refs_2_ = bf16[576,1152]{1,0:T(8,128)(2,1)S(1)} collective-permute-done((bf16[576,1152]{1,0:T(8,128)(2,1)S(1)}, bf16[576,1152]{1,0:T(8,128)(2,1)S(1)}, u32[]{:S(2)}, u32[]{:S(2)}) %collective-permute-start.36) | collective-permute-done | bytes 1327136 | tf_op jit(solution)/shard_map/ppermute | solution.py:35
  403.3 31.8 %collective-permute-done.37.refs_3_ = bf16[576,1152]{1,0:T(8,128)(2,1)S(1)} collective-permute-done((bf16[576,1152]{1,0:T(8,128)(2,1)}, bf16[576,1152]{1,0:T(8,128)(2,1)S(1)}, u32[]{:S(2)}, u32[]{:S(2)}) %collective-permute-start.37) | collective-permute-done | bytes 1327136 | tf_op jit(solution)/shard_map/ppermute | solution.py:35
  439.4 46.9 %shard_map.84 = (bf16[2048,2304]{1,0:T(8,128)(2,1)}, bf16[2048,2304]{1,0:T(8,128)(2,1)}, bf16[8,288,2304]{2,1,0:T(8,128)(2,1)}) custom-call(s32[16]{0:T(128)} %stack.94.pos, bf16[2048,1152]{1,0:T(8,128)(2,1)} %bitcast.67, f32[2048,2304]{1,0:T(8,128)} %get-tuple-element.55.s_ref, f32[2048,2304]{1,0:T(8,128)} %get-tuple-element.56.t_ref, ...), custom_call_target="tpu_custom_call" | custom-call | flops 32614907904 | bytes 85000000 | tf_op jit(solution)/shard_map/pallas_call | solution.py:266
  486.3 46.5 %shard_map.85 = (bf16[2048,2304]{1,0:T(8,128)(2,1)}, bf16[2048,2304]{1,0:T(8,128)(2,1)}, bf16[8,288,2304]{2,1,0:T(8,128)(2,1)}) custom-call(s32[16]{0:T(128)} %stack.94.pos, bf16[2048,1152]{1,0:T(8,128)(2,1)} %bitcast.68, f32[2048,2304]{1,0:T(8,128)} %get-tuple-element.62.s_ref, f32[2048,2304]{1,0:T(8,128)} %get-tuple-element.63.t_ref, ...), custom_call_target="tpu_custom_call" | custom-call | flops 32614907904 | bytes 85000000 | tf_op jit(solution)/shard_map/pallas_call | solution.py:266
  532.8 35.5 %shard_map.86.refs_0_ = bf16[2048,1152]{1,0:T(8,128)(2,1)} custom-call(s32[16]{0:T(128)} %stack.94.pos, bf16[2048,2304]{1,0:T(8,128)(2,1)} %get-tuple-element.65.ga, bf16[2048,2304]{1,0:T(8,128)(2,1)} %get-tuple-element.66.gb, bf16[288,2304]{1,0:T(8,128)(2,1)} %copy-done.9, bf16[288,2304]{1,0:T(8,128)(2,1)} %collective-permute-done.21.refs_1_.refs_4_, ...), custom_call_target="tpu_custom_call" | custom-call | flops 21743271936 | bytes 45000000 | tf_op jit(solution)/shard_map/pallas_call | solution.py:327
  568.4 41.5 %shard_map.87.dh_ref.refs_2_ = bf16[2048,1152]{1,0:T(8,128)(2,1)} custom-call(s32[16]{0:T(128)} %stack.94.pos, bf16[2048,2304]{1,0:T(8,128)(2,1)} %get-tuple-element.59.ga, bf16[2048,2304]{1,0:T(8,128)(2,1)} %get-tuple-element.64.gb, bf16[2048,1152]{1,0:T(8,128)(2,1)} %shard_map.86.refs_0_, bf16[2048,1152]{1,0:T(8,128)(2,1)} %get-tuple-element.67.refs_1_, ...), custom_call_target="tpu_custom_call" | custom-call | flops 21743271936 | bytes 45000000 | tf_op jit(solution)/shard_map/pallas_call | solution.py:327
  609.9 32.2 %by_down.3 = bf16[4608,1152]{1,0:T(8,128)(2,1)} custom-call(bf16[2048,2304]{1,0:T(8,128)(2,1)} %get-tuple-element.44.aa, bf16[2048,2304]{1,0:T(8,128)(2,1)} %get-tuple-element.46.ab, bf16[2048,1152]{1,0:T(8,128)(2,1)} %shard_map.87.dh_ref.refs_2_), custom_call_target="tpu_custom_call" | custom-call | flops 21743271936 | bytes 35000000 | tf_op jit(solution)/shard_map/by_down/pallas_call | solution.py:214
  643.5 50.7 %shard_map.88 = (bf16[2048,2304]{1,0:T(8,128)(2,1)}, bf16[2048,2304]{1,0:T(8,128)(2,1)}, bf16[8,288,2304]{2,1,0:T(8,128)(2,1)}) custom-call(s32[16]{0:T(128)} %stack.94.pos, bf16[2048,1152]{1,0:T(8,128)(2,1)} %shard_map.87.dh_ref.refs_2_, f32[2048,2304]{1,0:T(8,128)} %get-tuple-element.69.s_ref, f32[2048,2304]{1,0:T(8,128)} %get-tuple-element.70.t_ref, ...), custom_call_target="tpu_custom_call" | custom-call | flops 32614907904 | bytes 85000000 | tf_op jit(solution)/shard_map/pallas_call | solution.py:266
  694.3 48.5 %shard_map.89 = (bf16[2048,2304]{1,0:T(8,128)(2,1)}, bf16[2048,2304]{1,0:T(8,128)(2,1)}, bf16[8,288,2304]{2,1,0:T(8,128)(2,1)}) custom-call(s32[16]{0:T(128)} %stack.94.pos, bf16[2048,1152]{1,0:T(8,128)(2,1)} %shard_map.87.dh_ref.refs_2_, f32[2048,2304]{1,0:T(8,128)} %get-tuple-element.75.s_ref, f32[2048,2304]{1,0:T(8,128)} %get-tuple-element.76.t_ref, ...), custom_call_target="tpu_custom_call" | custom-call | flops 32614907904 | bytes 85000000 | tf_op jit(solution)/shard_map/pallas_call | solution.py:266
  742.8 2.8 slice.118
  745.7 8.6 collective-permute-done.42
  754.4 5.4 fusion.3
  759.8 35.7 %shard_map.90.refs_0_ = bf16[2048,1152]{1,0:T(8,128)(2,1)} custom-call(s32[16]{0:T(128)} %stack.94.pos, bf16[2048,2304]{1,0:T(8,128)(2,1)} %get-tuple-element.78.ga, bf16[2048,2304]{1,0:T(8,128)(2,1)} %get-tuple-element.79.gb, bf16[288,2304]{1,0:T(8,128)(2,1)} %copy-done.5, bf16[288,2304]{1,0:T(8,128)(2,1)} %collective-permute-done.refs_1_.refs_4_, ...), custom_call_target="tpu_custom_call" | custom-call | flops 21743271936 | bytes 45000000 | tf_op jit(solution)/shard_map/pallas_call | solution.py:327
  800.4 42.3 %shard_map.91 = bf16[2048,1152]{1,0:T(8,128)(2,1)} custom-call(s32[16]{0:T(128)} %stack.94.pos, bf16[2048,2304]{1,0:T(8,128)(2,1)} %get-tuple-element.72.ga, bf16[2048,2304]{1,0:T(8,128)(2,1)} %get-tuple-element.77.gb, bf16[2048,1152]{1,0:T(8,128)(2,1)} %shard_map.90.refs_0_, bf16[2048,1152]{1,0:T(8,128)(2,1)} %bitcast.63, ...), custom_call_target="tpu_custom_call" | custom-call | flops 21743271936 | bytes 45000000 | tf_op jit(solution)/shard_map/pallas_call | solution.py:327
  846.0 3.5 pad_maximum_fusion.2
  851.7 28.2 %reduce-scatter.8.cloned.1.call-done = bf16[288,2304]{1,0:T(8,128)(2,1)} async-done(((bf16[2304,2304]{1,0:T(8,128)(2,1)}), bf16[288,2304]{1,0:T(8,128)(2,1)}) %reduce-scatter.8.cloned.1.call-update) | async-done | bytes 1327120 | tf_op jit(solution)/shard_map/reduce_scatter | solution.py:367
  882.5 75.0 %reduce-scatter.6.cloned.1.call-done = bf16[288,2304]{1,0:T(8,128)(2,1)} async-done(((bf16[2304,2304]{1,0:T(8,128)(2,1)}), bf16[288,2304]{1,0:T(8,128)(2,1)}) %reduce-scatter.6.cloned.1.call-update) | async-done | bytes 1327120 | tf_op jit(solution)/shard_map/reduce_scatter | solution.py:367
  (166 shorter events, 60.7 us)
Async XLA Ops:
  7.2 838.8 %reduce-scatter.14.cloned.1.call-start = ((), (), s32[]{:S(2)}) async-start(), calls=%async_computation.9 | async-start | bytes 11943936 | tf_op jit(solution)/shard_map/reduce_scatter | solution.py:367
  46.6 57.1 %collective-permute-start.8 = (bf16[288,2304]{1,0:T(8,128)(2,1)S(1)}, bf16[288,2304]{1,0:T(8,128)(2,1)}, u32[]{:S(2)}, u32[]{:S(2)}) collective-permute-start(bf16[288,2304]{1,0:T(8,128)(2,1)S(1)} %pad_maximum_fusion.4.refs_0_.refs_8_.refs_11_), channel_id=1, source_target_pairs={{0,2},{1,5},{2,0},{3,7},{4,6},{5,1},{6,4},{7,3}} | collective-permute-start | bytes 3981320 | tf_op jit(solution)/shard_map/ppermute | solution.py:35
  46.9 59.4 %collective-permute-start.7 = (bf16[288,2304]{1,0:T(8,128)(2,1)S(1)}, bf16[288,2304]{1,0:T(8,128)(2,1)}, u32[]{:S(2)}, u32[]{:S(2)}) collective-permute-start(bf16[288,2304]{1,0:T(8,128)(2,1)S(1)} %pad_maximum_fusion.4.refs_0_.refs_8_.refs_11_), channel_id=1, source_target_pairs={{0,4},{1,3},{2,6},{3,1},{4,0},{5,7},{6,2},{7,5}} | collective-permute-start | bytes 3981320 | tf_op jit(solution)/shard_map/ppermute | solution.py:35
  77.9 52.3 %collective-permute-start.2 = (bf16[288,2304]{1,0:T(8,128)(2,1)}, bf16[288,2304]{1,0:T(8,128)(2,1)}, u32[]{:S(2)}, u32[]{:S(2)}) collective-permute-start(bf16[288,2304]{1,0:T(8,128)(2,1)} %collective-permute-done.refs_1_.refs_4_), channel_id=1, source_target_pairs={{0,2},{1,5},{2,0},{3,7},{4,6},{5,1},{6,4},{7,3}} | collective-permute-start | bytes 3981320 | tf_op jit(solution)/shard_map/ppermute | solution.py:35
  77.9 68.4 %collective-permute-start.29 = (bf16[288,2304]{1,0:T(8,128)(2,1)S(1)}, bf16[288,2304]{1,0:T(8,128)(2,1)S(1)}, u32[]{:S(2)}, u32[]{:S(2)}) collective-permute-start(bf16[288,2304]{1,0:T(8,128)(2,1)S(1)} %pad_maximum_fusion.6.refs_0_.refs_8_.refs_11_), channel_id=1, source_target_pairs={{0,2},{1,5},{2,0},{3,7},{4,6},{5,1},{6,4},{7,3}} | collective-permute-start | bytes 3981320 | tf_op jit(solution)/shard_map/ppermute | solution.py:35
  103.7 42.6 %collective-permute-start.28 = (bf16[288,2304]{1,0:T(8,128)(2,1)S(1)}, bf16[288,2304]{1,0:T(8,128)(2,1)S(1)}, u32[]{:S(2)}, u32[]{:S(2)}) collective-permute-start(bf16[288,2304]{1,0:T(8,128)(2,1)S(1)} %pad_maximum_fusion.6.refs_0_.refs_8_.refs_11_), channel_id=1, source_target_pairs={{0,4},{1,3},{2,6},{3,1},{4,0},{5,7},{6,2},{7,5}} | collective-permute-start | bytes 3981320 | tf_op jit(solution)/shard_map/ppermute | solution.py:35
  106.3 50.1 %collective-permute-start.12 = (bf16[288,2304]{1,0:T(8,128)(2,1)}, bf16[288,2304]{1,0:T(8,128)(2,1)}, u32[]{:S(2)}, u32[]{:S(2)}) collective-permute-start(bf16[288,2304]{1,0:T(8,128)(2,1)} %collective-permute-done.8.refs_2_.refs_10_.refs_13_), channel_id=1, source_target_pairs={{0,1},{1,0},{2,3},{3,2},{4,5},{5,4},{6,7},{7,6}} | collective-permute-start | bytes 3981320 | tf_op jit(solution)/shard_map/ppermute | solution.py:35
  106.3 54.3 %collective-permute-start.9 = (bf16[288,2304]{1,0:T(8,128)(2,1)}, bf16[288,2304]{1,0:T(8,128)(2,1)}, u32[]{:S(2)}, u32[]{:S(2)}) collective-permute-start(bf16[288,2304]{1,0:T(8,128)(2,1)} %collective-permute-done.7.refs_1_.refs_9_.refs_12_), channel_id=1, source_target_pairs={{0,2},{1,5},{2,0},{3,7},{4,6},{5,1},{6,4},{7,3}} | collective-permute-start | bytes 3981320 | tf_op jit(solution)/shard_map/ppermute | solution.py:35
  156.5 42.6 %collective-permute-start.22 = (bf16[288,2304]{1,0:T(8,128)(2,1)S(1)}, bf16[288,2304]{1,0:T(8,128)(2,1)}, u32[]{:S(2)}, u32[]{:S(2)}) collective-permute-start(bf16[288,2304]{1,0:T(8,128)(2,1)S(1)} %pad_maximum_fusion.5.refs_0_.refs_3_), channel_id=1, source_target_pairs={{0,2},{1,5},{2,0},{3,7},{4,6},{5,1},{6,4},{7,3}} | collective-permute-start | bytes 3981320 | tf_op jit(solution)/shard_map/ppermute | solution.py:35
  160.6 39.0 %collective-permute-start.21 = (bf16[288,2304]{1,0:T(8,128)(2,1)S(1)}, bf16[288,2304]{1,0:T(8,128)(2,1)}, u32[]{:S(2)}, u32[]{:S(2)}) collective-permute-start(bf16[288,2304]{1,0:T(8,128)(2,1)S(1)} %pad_maximum_fusion.5.refs_0_.refs_3_), channel_id=1, source_target_pairs={{0,4},{1,3},{2,6},{3,1},{4,0},{5,7},{6,2},{7,5}} | collective-permute-start | bytes 3981320 | tf_op jit(solution)/shard_map/ppermute | solution.py:35
  162.2 41.1 %collective-permute-start.16 = (bf16[576,1152]{1,0:T(8,128)(2,1)}, bf16[576,1152]{1,0:T(8,128)(2,1)}, u32[]{:S(2)}, u32[]{:S(2)}) collective-permute-start(bf16[576,1152]{1,0:T(8,128)(2,1)} %collective-permute-done.14.refs_1_), channel_id=1, source_target_pairs={{0,2},{1,5},{2,0},{3,7},{4,6},{5,1},{6,4},{7,3}} | collective-permute-start | bytes 3981320 | tf_op jit(solution)/shard_map/ppermute | solution.py:35
  199.1 39.1 %collective-permute-start.17 = (bf16[576,1152]{1,0:T(8,128)(2,1)S(1)}, bf16[576,1152]{1,0:T(8,128)(2,1)}, u32[]{:S(2)}, u32[]{:S(2)}) collective-permute-start(bf16[576,1152]{1,0:T(8,128)(2,1)S(1)} %copy-done.11), channel_id=1, source_target_pairs={{0,1},{1,0},{2,3},{3,2},{4,5},{5,4},{6,7},{7,6}} | collective-permute-start | bytes 3981320 | tf_op jit(solution)/shard_map/ppermute | solution.py:35
  199.6 39.1 %collective-permute-start.19 = (bf16[576,1152]{1,0:T(8,128)(2,1)}, bf16[576,1152]{1,0:T(8,128)(2,1)}, u32[]{:S(2)}, u32[]{:S(2)}) collective-permute-start(bf16[576,1152]{1,0:T(8,128)(2,1)} %copy-done.15), channel_id=1, source_target_pairs={{0,1},{1,0},{2,3},{3,2},{4,5},{5,4},{6,7},{7,6}} | collective-permute-start | bytes 3981320 | tf_op jit(solution)/shard_map/ppermute | solution.py:35
  199.7 39.6 %collective-permute-start.18 = (bf16[576,1152]{1,0:T(8,128)(2,1)}, bf16[576,1152]{1,0:T(8,128)(2,1)}, u32[]{:S(2)}, u32[]{:S(2)}) collective-permute-start(bf16[576,1152]{1,0:T(8,128)(2,1)} %collective-permute-done.14.refs_1_), channel_id=1, source_target_pairs={{0,1},{1,0},{2,3},{3,2},{4,5},{5,4},{6,7},{7,6}} | collective-permute-start | bytes 3981320 | tf_op jit(solution)/shard_map/ppermute | solution.py:35
  200.1 38.6 %collective-permute-start.23 = (bf16[288,2304]{1,0:T(8,128)(2,1)}, bf16[288,2304]{1,0:T(8,128)(2,1)}, u32[]{:S(2)}, u32[]{:S(2)}) collective-permute-start(bf16[288,2304]{1,0:T(8,128)(2,1)} %collective-permute-done.21.refs_1_.refs_4_), channel_id=1, source_target_pairs={{0,2},{1,5},{2,0},{3,7},{4,6},{5,1},{6,4},{7,3}} | collective-permute-start | bytes 3981320 | tf_op jit(solution)/shard_map/ppermute | solution.py:35
  238.2 40.2 %collective-permute-start.24 = (bf16[288,2304]{1,0:T(8,128)(2,1)S(1)}, bf16[288,2304]{1,0:T(8,128)(2,1)}, u32[]{:S(2)}, u32[]{:S(2)}) collective-permute-start(bf16[288,2304]{1,0:T(8,128)(2,1)S(1)} %pad_maximum_fusion.5.refs_0_.refs_3_), channel_id=1, source_target_pairs={{0,1},{1,0},{2,3},{3,2},{4,5},{5,4},{6,7},{7,6}} | collective-permute-start | bytes 3981320 | tf_op jit(solution)/shard_map/ppermute | solution.py:35
  238.7 41.7 %collective-permute-start.25 = (bf16[288,2304]{1,0:T(8,128)(2,1)}, bf16[288,2304]{1,0:T(8,128)(2,1)}, u32[]{:S(2)}, u32[]{:S(2)}) collective-permute-start(bf16[288,2304]{1,0:T(8,128)(2,1)} %collective-permute-done.21.refs_1_.refs_4_), channel_id=1, source_target_pairs={{0,1},{1,0},{2,3},{3,2},{4,5},{5,4},{6,7},{7,6}} | collective-permute-start | bytes 3981320 | tf_op jit(solution)/shard_map/ppermute | solution.py:35
  238.8 40.1 %collective-permute-start.26 = (bf16[288,2304]{1,0:T(8,128)(2,1)}, bf16[288,2304]{1,0:T(8,128)(2,1)}, u32[]{:S(2)}, u32[]{:S(2)}) collective-permute-start(bf16[288,2304]{1,0:T(8,128)(2,1)} %collective-permute-done.22.refs_2_.refs_5_), channel_id=1, source_target_pairs={{0,1},{1,0},{2,3},{3,2},{4,5},{5,4},{6,7},{7,6}} | collective-permute-start | bytes 3981320 | tf_op jit(solution)/shard_map/ppermute | solution.py:35
  239.2 41.7 %collective-permute-start.30 = (bf16[288,2304]{1,0:T(8,128)(2,1)}, bf16[288,2304]{1,0:T(8,128)(2,1)}, u32[]{:S(2)}, u32[]{:S(2)}) collective-permute-start(bf16[288,2304]{1,0:T(8,128)(2,1)} %copy-done.17), channel_id=1, source_target_pairs={{0,2},{1,5},{2,0},{3,7},{4,6},{5,1},{6,4},{7,3}} | collective-permute-start | bytes 3981320 | tf_op jit(solution)/shard_map/ppermute | solution.py:35
  241.0 39.5 %collective-permute-start.27 = (bf16[288,2304]{1,0:T(8,128)(2,1)}, bf16[288,2304]{1,0:T(8,128)(2,1)}, u32[]{:S(2)}, u32[]{:S(2)}) collective-permute-start(bf16[288,2304]{1,0:T(8,128)(2,1)} %collective-permute-done.23.refs_3_.refs_6_), channel_id=1, source_target_pairs={{0,1},{1,0},{2,3},{3,2},{4,5},{5,4},{6,7},{7,6}} | collective-permute-start | bytes 3981320 | tf_op jit(solution)/shard_map/ppermute | solution.py:35
  278.4 37.8 %collective-permute-start.31 = (bf16[288,2304]{1,0:T(8,128)(2,1)S(1)}, bf16[288,2304]{1,0:T(8,128)(2,1)S(1)}, u32[]{:S(2)}, u32[]{:S(2)}) collective-permute-start(bf16[288,2304]{1,0:T(8,128)(2,1)S(1)} %copy-done.8), channel_id=1, source_target_pairs={{0,1},{1,0},{2,3},{3,2},{4,5},{5,4},{6,7},{7,6}} | collective-permute-start | bytes 3981320 | tf_op jit(solution)/shard_map/ppermute | solution.py:35
  278.9 106.9 %collective-permute-start.35 = (bf16[576,1152]{1,0:T(8,128)(2,1)}, bf16[576,1152]{1,0:T(8,128)(2,1)}, u32[]{:S(2)}, u32[]{:S(2)}) collective-permute-start(bf16[576,1152]{1,0:T(8,128)(2,1)} %get-tuple-element.58.refs_0_), channel_id=1, source_target_pairs={{0,4},{1,3},{2,6},{3,1},{4,0},{5,7},{6,2},{7,5}} | collective-permute-start | bytes 3981320 | tf_op jit(solution)/shard_map/ppermute | solution.py:35
  384.2 461.8 %reduce-scatter.12.cloned.1.call-start = ((), (), s32[]{:S(2)}) async-start(), calls=%async_computation.8 | async-start | bytes 11943936 | tf_op jit(solution)/shard_map/reduce_scatter | solution.py:367
  385.8 49.3 %collective-permute-start.37 = (bf16[576,1152]{1,0:T(8,128)(2,1)}, bf16[576,1152]{1,0:T(8,128)(2,1)S(1)}, u32[]{:S(2)}, u32[]{:S(2)}) collective-permute-start(bf16[576,1152]{1,0:T(8,128)(2,1)} %collective-permute-done.35.refs_1_), channel_id=1, source_target_pairs={{0,2},{1,5},{2,0},{3,7},{4,6},{5,1},{6,4},{7,3}} | collective-permute-start | bytes 3981320 | tf_op jit(solution)/shard_map/ppermute | solution.py:35
  387.6 47.6 %collective-permute-start.38 = (bf16[576,1152]{1,0:T(8,128)(2,1)S(1)}, bf16[576,1152]{1,0:T(8,128)(2,1)S(1)}, u32[]{:S(2)}, u32[]{:S(2)}) collective-permute-start(bf16[576,1152]{1,0:T(8,128)(2,1)S(1)} %copy-done.12), channel_id=1, source_target_pairs={{0,1},{1,0},{2,3},{3,2},{4,5},{5,4},{6,7},{7,6}} | collective-permute-start | bytes 3981320 | tf_op jit(solution)/shard_map/ppermute | solution.py:35
  387.6 48.7 %collective-permute-start.39 = (bf16[576,1152]{1,0:T(8,128)(2,1)}, bf16[576,1152]{1,0:T(8,128)(2,1)S(1)}, u32[]{:S(2)}, u32[]{:S(2)}) collective-permute-start(bf16[576,1152]{1,0:T(8,128)(2,1)} %collective-permute-done.35.refs_1_), channel_id=1, source_target_pairs={{0,1},{1,0},{2,3},{3,2},{4,5},{5,4},{6,7},{7,6}} | collective-permute-start | bytes 3981320 | tf_op jit(solution)/shard_map/ppermute | solution.py:35
  642.2 207.3 %reduce-scatter.10.cloned.1.call-start = ((), (), s32[]{:S(2)}) async-start(), calls=%async_computation.7 | async-start | bytes 11943936 | tf_op jit(solution)/shard_map/reduce_scatter | solution.py:367
  642.9 237.0 %reduce-scatter.8.cloned.1.call-start = ((), (), s32[]{:S(2)}) async-start(), calls=%async_computation.6 | async-start | bytes 11943936 | tf_op jit(solution)/shard_map/reduce_scatter | solution.py:367
  643.5 314.0 %reduce-scatter.6.cloned.1.call-start = ((), (), s32[]{:S(2)}) async-start(), calls=%async_computation.5 | async-start | bytes 11943936 | tf_op jit(solution)/shard_map/reduce_scatter | solution.py:367
  759.8 37.7 %collective-permute-start.44 = (bf16[288,2304]{1,0:T(8,128)(2,1)S(1)}, bf16[288,2304]{1,0:T(8,128)(2,1)S(1)}, u32[]{:S(2)}, u32[]{:S(2)}) collective-permute-start(bf16[288,2304]{1,0:T(8,128)(2,1)S(1)} %get-tuple-element.83), channel_id=1, source_target_pairs={{0,4},{1,3},{2,6},{3,1},{4,0},{5,7},{6,2},{7,5}} | collective-permute-start | bytes 3981320 | tf_op jit(solution)/shard_map/ppermute | solution.py:35
  795.5 47.2 %collective-permute-start.43 = (bf16[288,2304]{1,0:T(8,128)(2,1)}, bf16[288,2304]{1,0:T(8,128)(2,1)S(1)}, u32[]{:S(2)}, u32[]{:S(2)}) collective-permute-start(bf16[288,2304]{1,0:T(8,128)(2,1)} %get-tuple-element.82), channel_id=1, source_target_pairs={{0,4},{1,3},{2,6},{3,1},{4,0},{5,7},{6,2},{7,5}} | collective-permute-start | bytes 3981320 | tf_op jit(solution)/shard_map/ppermute | solution.py:35
  799.8 42.9 %collective-permute-start.45 = (bf16[288,2304]{1,0:T(8,128)(2,1)S(1)}, bf16[288,2304]{1,0:T(8,128)(2,1)S(1)}, u32[]{:S(2)}, u32[]{:S(2)}) collective-permute-start(bf16[288,2304]{1,0:T(8,128)(2,1)S(1)} %fusion), channel_id=1, source_target_pairs={{0,2},{1,5},{2,0},{3,7},{4,6},{5,1},{6,4},{7,3}} | collective-permute-start | bytes 3981320 | tf_op jit(solution)/shard_map/ppermute | solution.py:35
  (44 other events, 1089.1 us)
Sparse Core Ops, SparseCore 0:
  384.4 83.4 reduce-scatter.13
  642.3 73.4 reduce-scatter.11
  719.2 82.8 reduce-scatter.9
  805.3 74.4 reduce-scatter.7
  883.2 74.2 reduce-scatter.5

commit v2 on v1

--- a/solution.py
+++ b/solution.py
@@ -13,7 +13,7 @@
 RD = D // 8
 RF = FF // 8
 BF, F32 = jnp.bfloat16, jnp.float32
-VMEM_LIMIT = 60 * 1024 * 1024
+VMEM_LIMIT = 67_043_328
 NT = (((1,), (1,)), ((), ()))
 TN = (((0,), (0,)), ((), ()))
 ANY = pl.BlockSpec(memory_space=pl.ANY)
@@ -64,7 +64,7 @@
     return jnp.stack([v.astype(jnp.int32) for v in (*where, *slots)])
 
 
-GU_M, GU_N, GU_C = 512, 768, 128
+GU_M, GU_N, GU_C = 512, 768, 512
 GU_STEPS = HALF // GU_N
 
 
@@ -245,7 +245,14 @@
     @pl.when(n == 0)
     def _():
         each(lambda c: c.start())
-        each(lambda c: c.wait())
+
+    for j, b in enumerate(blocks):
+        k = pos[j] - 4 * half
+
+        @pl.when((k >= 0) & (k < 4) & (n == k * RF // BG_N))
+        def _():
+            rows = pl.ds(pl.multiple_of(k * RF, 16), RF)
+            pltpu.make_async_copy(b, wd.at[rows, :], sem.at[j]).wait()
 
     w = wd[pl.ds(pl.multiple_of(n * BG_N, BG_N), BG_N), :]
     for c in range(0, T, BG_C):
@@ -339,6 +346,33 @@
     )(pos, ga, gb, *extra, *blocks_a, *blocks_b)
 
 
+def lay_body(*refs):
+    pieces, (g_ref, u_ref, d_ref) = refs[:6], refs[6:]
+    for layer in range(2):
+
+        @pl.when(pl.program_id(0) == 1 - layer)
+        def _():
+            for half in range(2):
+                piece = pieces[3 * layer + half]
+                g_ref[0, :, half * HALF : (half + 1) * HALF] = piece[:RD]
+                u_ref[0, :, half * HALF : (half + 1) * HALF] = piece[RD:]
+            d_ref[0] = pieces[3 * layer + 2][...]
+
+
+def lay(pieces):
+    out = lambda rows, cols: pl.BlockSpec((1, rows, cols), lambda i: (1 - i, 0, 0))
+    return pl.pallas_call(
+        lay_body,
+        grid=(2,),
+        in_specs=[pl.BlockSpec(p.shape, lambda i: (0, 0)) for p in pieces],
+        out_specs=[out(RD, FF), out(RD, FF), out(RF, D)],
+        out_shape=[jax.ShapeDtypeStruct((2, *s), BF) for s in ((RD, FF), (RD, FF), (RF, D))],
+        compiler_params=params(),
+        cost_estimate=cost(1_000_000, 16_000_000),
+        name="lay",
+    )(*pieces)
+
+
 def after(v, *others):
     return lax.optimization_barrier((v, *others))[0]
 
@@ -354,8 +388,7 @@
 
 
 def by_hand(terms):
-    own, part = terms[:4], terms[4:]
-    got = send(part, partner)
+    own, got = terms[:4], send(terms, partner)[4:]
     pair = lambda k: own[k].astype(F32) + got[k].astype(F32)
     across = send(pair(1).astype(BF), first)
     one = send(pair(2).astype(BF), first)
@@ -397,18 +430,16 @@
         def backward(i, dh, h, at, acts, s, t, ga, gb, d):
             by_d = by_down(*acts, dh)
             later = after(dh, by_d)
-            dga, dua, by_ga = by_gate_up(pos, 0, False, later, s[0], t[0], at, d)
+            dga, dua, by_ga = by_gate_up(pos, 0, i == 0, later, s[0], t[0], at, d)
             later = after(later, by_ga)
-            dgb, dub, by_gb = by_gate_up(pos, 1, i == 0, later, s[1], t[1], at, d)
+            dgb, dub, by_gb = by_gate_up(pos, 1, False, later, s[1], t[1], at, d)
             da = by_a(pos, 0, dga, dgb, ga, gb)
             dh = by_a(pos, 1, dua, dub, ga, gb, (da, h, dh))
-            return dh, (scatter(by_d), scatter(by_ga), scatter(by_gb) if i else by_hand(by_gb))
+            return dh, (scatter(by_d), scatter(by_ga) if i else by_hand(by_ga), scatter(by_gb))
 
         dh, (gd1, gg1a, gg1b) = backward(1, dy, h1, at1, (act1a, act1b), (s1a, s1b), (t1a, t1b), g1a, g1b, d1)
         dx, (gd0, gg0a, gg0b) = backward(0, dh, x, at0, (act0a, act0b), (s0a, s0b), (t0a, t0b), g0a, g0b, d0)
-        by_gate = jnp.stack([jnp.concatenate([p[:RD], q[:RD]], 1) for p, q in ((gg0a, gg0b), (gg1a, gg1b))])
-        by_up = jnp.stack([jnp.concatenate([p[RD:], q[RD:]], 1) for p, q in ((gg0a, gg0b), (gg1a, gg1b))])
-        return dx[None], by_gate, by_up, jnp.stack([gd0, gd1])
+        return dx[None], *lay((gg0a, gg0b, gd0, gg1a, gg1b, gd1))
 
     tokens, rows = P(("rep", "dp"), None, None), P(None, "dp", None)
     return jax.shard_map(

time: 973 us -> 1060 us (1.089)
  waiting for transfers between devices: 288 us -> 388 us
  local copies, waits for them, and re-layouts: 20.4 us -> 7.39 us
    reduce_scatter x5, waiting for transfers between devices: 103 us -> 213 us  [scatter(): lax.psum_scatter(terms.reshape(-1, terms.shape[-1]), 'dp', scatter_dimens...]
  transfers between devices with their start and end apart: 51 -> 51, of which waited for: 15 -> 14; matrix products, arithmetic and copies ran while one was open for 2% -> 2% of each run, Pallas kernels for 62% -> 56%
where the time goes in v2:
time: 1060 us
  Pallas kernels  598 us (56%)
  waiting for transfers between devices  388 us (37%)
  starting transfers between devices  33.2 us (3%)
  other arithmetic  16.3 us (2%)
  between operations  14.4 us (1%)
    reduce_scatter x5, waiting for transfers between devices, scatter(): lax.psum_scatter(terms.reshape(-1, terms.shape[-1]), 'dp', scatter_dimens...  213 us
    pallas_call x4, Pallas kernels, by_gate_up(): pl.pallas_call(functools.partial(by_gate_up_body, half, slots), grid_spec...  190 us
    ppermute x46, waiting for transfers between devices, send(): return lax.ppermute(v, 'dp', [(i, to(i)) for i in range(8)])  174 us
    pallas_call x4, Pallas kernels, by_a(): pl.pallas_call(functools.partial(by_a_body, part), grid_spec=pltpu.Prefet...  154 us
    pallas_call x4, Pallas kernels, gate_up(): pl.pallas_call(gu_body, grid_spec=pltpu.PrefetchScalarGridSpec(num_scalar...  138 us
    pallas_call x2, Pallas kernels, by_down(): pl.pallas_call(by_down_body, grid=(4,), in_specs=[pl.BlockSpec((T, D), la...  64.4 us
    pallas_call x1, Pallas kernels, down(): pl.pallas_call(down_body, grid_spec=pltpu.PrefetchScalarGridSpec(num_scal...  37.2 us
    ppermute x46, starting transfers between devices, send(): return lax.ppermute(v, 'dp', [(i, to(i)) for i in range(8)])  33 us
  transfers between devices with their start and end apart: 51, of which 14 were waited for; matrix products, arithmetic and copies ran while one was open for 2% of the time, Pallas kernels for 56%

profile of v2, /device:TPU:0, one launch (start us, length us, event | category | flops | bytes accessed | tf_op | source)
XLA Modules:
  0.0 1057.3 jit_solution(8147359324978518118)
XLA Ops:
  18.7 24.5 %collective-permute-done.1.refs_2_.refs_5_ = bf16[288,2304]{1,0:T(8,128)(2,1)} collective-permute-done((bf16[288,2304]{1,0:T(8,128)(2,1)S(1)}, bf16[288,2304]{1,0:T(8,128)(2,1)}, u32[]{:S(2)}, u32[]{:S(2)}) %collective-permute-start.1) | collective-permute-done | bytes 1327136 | tf_op jit(solution)/shard_map/ppermute | solution.py:35
  47.8 23.8 %collective-permute-done.8.refs_2_.refs_10_.refs_13_ = bf16[288,2304]{1,0:T(8,128)(2,1)S(1)} collective-permute-done((bf16[288,2304]{1,0:T(8,128)(2,1)S(1)}, bf16[288,2304]{1,0:T(8,128)(2,1)S(1)}, u32[]{:S(2)}, u32[]{:S(2)}) %collective-permute-start.8) | collective-permute-done | bytes 1327136 | tf_op jit(solution)/shard_map/ppermute | solution.py:35
  74.3 25.8 %collective-permute-done.15.refs_2_ = bf16[576,1152]{1,0:T(8,128)(2,1)S(1)} collective-permute-done((bf16[576,1152]{1,0:T(8,128)(2,1)S(1)}, bf16[576,1152]{1,0:T(8,128)(2,1)S(1)}, u32[]{:S(2)}, u32[]{:S(2)}) %collective-permute-start.15) | collective-permute-done | bytes 1327136 | tf_op jit(solution)/shard_map/ppermute | solution.py:35
  105.6 26.2 %collective-permute-done.2.refs_3_.refs_6_ = bf16[288,2304]{1,0:T(8,128)(2,1)} collective-permute-done((bf16[288,2304]{1,0:T(8,128)(2,1)}, bf16[288,2304]{1,0:T(8,128)(2,1)}, u32[]{:S(2)}, u32[]{:S(2)}) %collective-permute-start.2) | collective-permute-done | bytes 1327136 | tf_op jit(solution)/shard_map/ppermute | solution.py:35
  131.8 15.2 %collective-permute-done.29.refs_2_.refs_10_.refs_13_ = bf16[288,2304]{1,0:T(8,128)(2,1)S(1)} collective-permute-done((bf16[288,2304]{1,0:T(8,128)(2,1)S(1)}, bf16[288,2304]{1,0:T(8,128)(2,1)S(1)}, u32[]{:S(2)}, u32[]{:S(2)}) %collective-permute-start.29) | collective-permute-done | bytes 1327136 | tf_op jit(solution)/shard_map/ppermute | solution.py:35
  149.1 7.8 norm.1
  156.8 4.5 collective-permute-done.22.refs_2_.refs_5_
  162.3 24.7 %collective-permute-done.9.refs_3_.refs_11_.refs_14_ = bf16[288,2304]{1,0:T(8,128)(2,1)} collective-permute-done((bf16[288,2304]{1,0:T(8,128)(2,1)}, bf16[288,2304]{1,0:T(8,128)(2,1)}, u32[]{:S(2)}, u32[]{:S(2)}) %collective-permute-start.9) | collective-permute-done | bytes 1327136 | tf_op jit(solution)/shard_map/ppermute | solution.py:35
  189.8 34.5 %gate_up.4 = (bf16[2048,2304]{1,0:T(8,128)(2,1)}, f32[2048,2304]{1,0:T(8,128)}, f32[2048,2304]{1,0:T(8,128)}) custom-call(s32[16]{0:T(128)} %stack.67.pos, bf16[2048,1152]{1,0:T(8,128)(2,1)} %get-tuple-element.48.a_ref, bf16[288,2304]{1,0:T(8,128)(2,1)} %copy-done.2, bf16[288,2304]{1,0:T(8,128)(2,1)} %collective-permute-done.refs_1_.refs_4_, ...), custom_call_target="tpu_custom_call" | custom-call | flops 21743271936 | bytes 70000000 | tf_op jit(solution)/shard_map/gate_up/pallas_call | solution.py:111
  225.8 34.5 %gate_up.5 = (bf16[2048,2304]{1,0:T(8,128)(2,1)}, f32[2048,2304]{1,0:T(8,128)}, f32[2048,2304]{1,0:T(8,128)}) custom-call(s32[16]{0:T(128)} %stack.67.pos, bf16[2048,1152]{1,0:T(8,128)(2,1)} %get-tuple-element.48.a_ref, bf16[288,2304]{1,0:T(8,128)(2,1)} %copy-done.3, bf16[288,2304]{1,0:T(8,128)(2,1)} %collective-permute-done.7.refs_1_.refs_9_.refs_12_, ...), custom_call_target="tpu_custom_call" | custom-call | flops 21743271936 | bytes 70000000 | tf_op jit(solution)/shard_map/gate_up/pallas_call | solution.py:111
  263.2 37.2 %down.1 = (bf16[2048,1152]{1,0:T(8,128)(2,1)}, bf16[2048,1152]{1,0:T(8,128)(2,1)}, bf16[1152,2048]{1,0:T(8,128)(2,1)}) custom-call(s32[16]{0:T(128)} %stack.67.pos, bf16[2048,2304]{1,0:T(8,128)(2,1)} %get-tuple-element.47.aa, bf16[2048,2304]{1,0:T(8,128)(2,1)} %get-tuple-element.49.ab, bf16[2048,1152]{1,0:T(8,128)(2,1)} %bitcast.52, ...), custom_call_target="tpu_custom_call" | custom-call | flops 21743271936 | bytes 45000000 | tf_op jit(solution)/shard_map/down/pallas_call | solution.py:185
  302.9 34.5 %gate_up.6 = (bf16[2048,2304]{1,0:T(8,128)(2,1)}, f32[2048,2304]{1,0:T(8,128)}, f32[2048,2304]{1,0:T(8,128)}) custom-call(s32[16]{0:T(128)} %stack.67.pos, bf16[2048,1152]{1,0:T(8,128)(2,1)} %get-tuple-element.54.a_ref, bf16[288,2304]{1,0:T(8,128)(2,1)} %pad_maximum_fusion.2.refs_0_.refs_3_, bf16[288,2304]{1,0:T(8,128)(2,1)} %collective-permute-done.21.refs_1_.refs_4_, ...), custom_call_target="tpu_custom_call" | custom-call | flops 21743271936 | bytes 70000000 | tf_op jit(solution)/shard_map/gate_up/pallas_call | solution.py:111
  338.5 34.6 %gate_up.7 = (bf16[2048,2304]{1,0:T(8,128)(2,1)}, f32[2048,2304]{1,0:T(8,128)}, f32[2048,2304]{1,0:T(8,128)}) custom-call(s32[16]{0:T(128)} %stack.67.pos, bf16[2048,1152]{1,0:T(8,128)(2,1)} %get-tuple-element.54.a_ref, bf16[288,2304]{1,0:T(8,128)(2,1)} %copy-done.4, bf16[288,2304]{1,0:T(8,128)(2,1)} %copy-done.14, bf16[288,2304]{1,0:T(8,128)(2,1)} %copy-done.13, ...), custom_call_target="tpu_custom_call" | custom-call | flops 21743271936 | bytes 70000000 | tf_op jit(solution)/shard_map/gate_up/pallas_call | solution.py:111
  373.2 32.1 %by_down.2 = bf16[4608,1152]{1,0:T(8,128)(2,1)} custom-call(bf16[2048,2304]{1,0:T(8,128)(2,1)} %get-tuple-element.53.aa, bf16[2048,2304]{1,0:T(8,128)(2,1)} %get-tuple-element.56.ab, bf16[2048,1152]{1,0:T(8,128)(2,1)} %bitcast.54), custom_call_target="tpu_custom_call" | custom-call | flops 21743271936 | bytes 35000000 | tf_op jit(solution)/shard_map/by_down/pallas_call | solution.py:214
  405.4 49.7 %shard_map.84 = (bf16[2048,2304]{1,0:T(8,128)(2,1)}, bf16[2048,2304]{1,0:T(8,128)(2,1)}, bf16[8,288,2304]{2,1,0:T(8,128)(2,1)}) custom-call(s32[16]{0:T(128)} %stack.67.pos, bf16[2048,1152]{1,0:T(8,128)(2,1)} %bitcast.55, f32[2048,2304]{1,0:T(8,128)} %get-tuple-element.58.s_ref, f32[2048,2304]{1,0:T(8,128)} %get-tuple-element.59.t_ref, ...), custom_call_target="tpu_custom_call" | custom-call | flops 32614907904 | bytes 85000000 | tf_op jit(solution)/shard_map/pallas_call | solution.py:273
  455.1 46.9 %shard_map.85 = (bf16[2048,2304]{1,0:T(8,128)(2,1)}, bf16[2048,2304]{1,0:T(8,128)(2,1)}, bf16[8,288,2304]{2,1,0:T(8,128)(2,1)}) custom-call(s32[16]{0:T(128)} %stack.67.pos, bf16[2048,1152]{1,0:T(8,128)(2,1)} %bitcast.56, f32[2048,2304]{1,0:T(8,128)} %get-tuple-element.65.s_ref, f32[2048,2304]{1,0:T(8,128)} %get-tuple-element.66.t_ref, ...), custom_call_target="tpu_custom_call" | custom-call | flops 32614907904 | bytes 85000000 | tf_op jit(solution)/shard_map/pallas_call | solution.py:273
  502.1 35.6 %shard_map.86.refs_0_ = bf16[2048,1152]{1,0:T(8,128)(2,1)} custom-call(s32[16]{0:T(128)} %stack.67.pos, bf16[2048,2304]{1,0:T(8,128)(2,1)} %get-tuple-element.68.ga, bf16[2048,2304]{1,0:T(8,128)(2,1)} %get-tuple-element.69.gb, bf16[288,2304]{1,0:T(8,128)(2,1)} %pad_maximum_fusion.2.refs_0_.refs_3_, ...), custom_call_target="tpu_custom_call" | custom-call | flops 21743271936 | bytes 45000000 | tf_op jit(solution)/shard_map/pallas_call | solution.py:334
  537.6 41.1 %shard_map.87.dh_ref.refs_2_ = bf16[2048,1152]{1,0:T(8,128)(2,1)} custom-call(s32[16]{0:T(128)} %stack.67.pos, bf16[2048,2304]{1,0:T(8,128)(2,1)} %get-tuple-element.62.ga, bf16[2048,2304]{1,0:T(8,128)(2,1)} %get-tuple-element.67.gb, bf16[2048,1152]{1,0:T(8,128)(2,1)} %shard_map.86.refs_0_, bf16[2048,1152]{1,0:T(8,128)(2,1)} %get-tuple-element.70.refs_1_, ...), custom_call_target="tpu_custom_call" | custom-call | flops 21743271936 | bytes 45000000 | tf_op jit(solution)/shard_map/pallas_call | solution.py:334
  578.7 32.3 %by_down.3 = bf16[4608,1152]{1,0:T(8,128)(2,1)} custom-call(bf16[2048,2304]{1,0:T(8,128)(2,1)} %get-tuple-element.47.aa, bf16[2048,2304]{1,0:T(8,128)(2,1)} %get-tuple-element.49.ab, bf16[2048,1152]{1,0:T(8,128)(2,1)} %shard_map.87.dh_ref.refs_2_), custom_call_target="tpu_custom_call" | custom-call | flops 21743271936 | bytes 35000000 | tf_op jit(solution)/shard_map/by_down/pallas_call | solution.py:214
  611.0 47.0 %shard_map.88 = (bf16[2048,2304]{1,0:T(8,128)(2,1)}, bf16[2048,2304]{1,0:T(8,128)(2,1)}, bf16[8,288,2304]{2,1,0:T(8,128)(2,1)}) custom-call(s32[16]{0:T(128)} %stack.67.pos, bf16[2048,1152]{1,0:T(8,128)(2,1)} %shard_map.87.dh_ref.refs_2_, f32[2048,2304]{1,0:T(8,128)} %get-tuple-element.72.s_ref, f32[2048,2304]{1,0:T(8,128)} %get-tuple-element.73.t_ref, ...), custom_call_target="tpu_custom_call" | custom-call | flops 32614907904 | bytes 85000000 | tf_op jit(solution)/shard_map/pallas_call | solution.py:273
  658.0 46.1 %shard_map.89 = (bf16[2048,2304]{1,0:T(8,128)(2,1)}, bf16[2048,2304]{1,0:T(8,128)(2,1)}, bf16[8,288,2304]{2,1,0:T(8,128)(2,1)}) custom-call(s32[16]{0:T(128)} %stack.67.pos, bf16[2048,1152]{1,0:T(8,128)(2,1)} %shard_map.87.dh_ref.refs_2_, f32[2048,2304]{1,0:T(8,128)} %get-tuple-element.78.s_ref, f32[2048,2304]{1,0:T(8,128)} %get-tuple-element.79.t_ref, ...), custom_call_target="tpu_custom_call" | custom-call | flops 32614907904 | bytes 85000000 | tf_op jit(solution)/shard_map/pallas_call | solution.py:273
  705.5 4.3 collective-permute-start.42
  709.8 23.9 %collective-permute-done.42 = bf16[8,288,2304]{2,1,0:T(8,128)(2,1)} collective-permute-done((bf16[8,288,2304]{2,1,0:T(8,128)(2,1)}, bf16[8,288,2304]{2,1,0:T(8,128)(2,1)}, u32[]{:S(2)}, u32[]{:S(2)}) %collective-permute-start.42) | collective-permute-done | bytes 10616864 | tf_op jit(solution)/shard_map/ppermute | solution.py:35
  733.7 4.7 fusion.3
  739.9 36.1 %shard_map.90.refs_0_ = bf16[2048,1152]{1,0:T(8,128)(2,1)} custom-call(s32[16]{0:T(128)} %stack.67.pos, bf16[2048,2304]{1,0:T(8,128)(2,1)} %get-tuple-element.81.ga, bf16[2048,2304]{1,0:T(8,128)(2,1)} %get-tuple-element.82.gb, bf16[288,2304]{1,0:T(8,128)(2,1)} %copy-done.2, bf16[288,2304]{1,0:T(8,128)(2,1)} %collective-permute-done.refs_1_.refs_4_, ...), custom_call_target="tpu_custom_call" | custom-call | flops 21743271936 | bytes 45000000 | tf_op jit(solution)/shard_map/pallas_call | solution.py:334
  778.1 4.5 fusion
  783.9 41.2 %shard_map.91 = bf16[2048,1152]{1,0:T(8,128)(2,1)} custom-call(s32[16]{0:T(128)} %stack.67.pos, bf16[2048,2304]{1,0:T(8,128)(2,1)} %get-tuple-element.75.ga, bf16[2048,2304]{1,0:T(8,128)(2,1)} %get-tuple-element.80.gb, bf16[2048,1152]{1,0:T(8,128)(2,1)} %shard_map.90.refs_0_, bf16[2048,1152]{1,0:T(8,128)(2,1)} %bitcast.53, ...), custom_call_target="tpu_custom_call" | custom-call | flops 21743271936 | bytes 45000000 | tf_op jit(solution)/shard_map/pallas_call | solution.py:334
  825.1 5.5 fusion.2.refs_0_
  830.6 58.1 %reduce-scatter.8.cloned.1.call-done.refs_2_ = bf16[576,1152]{1,0:T(8,128)(2,1)} async-done(((bf16[4608,1152]{1,0:T(8,128)(2,1)}), bf16[576,1152]{1,0:T(8,128)(2,1)}) %reduce-scatter.8.cloned.1.call-update) | async-done | bytes 1327120 | tf_op jit(solution)/shard_map/reduce_scatter | solution.py:400
  888.6 77.6 %reduce-scatter.12.cloned.1.call-done.refs_4_ = bf16[288,2304]{1,0:T(8,128)(2,1)} async-done(((bf16[2304,2304]{1,0:T(8,128)(2,1)}), bf16[288,2304]{1,0:T(8,128)(2,1)}) %reduce-scatter.12.cloned.1.call-update) | async-done | bytes 1327120 | tf_op jit(solution)/shard_map/reduce_scatter | solution.py:400
  966.2 77.6 %reduce-scatter.10.cloned.1.call-done.refs_3_ = bf16[288,2304]{1,0:T(8,128)(2,1)} async-done(((bf16[2304,2304]{1,0:T(8,128)(2,1)}), bf16[288,2304]{1,0:T(8,128)(2,1)}) %reduce-scatter.10.cloned.1.call-update) | async-done | bytes 1327120 | tf_op jit(solution)/shard_map/reduce_scatter | solution.py:400
  1043.8 6.8 lay.1
  (135 shorter events, 44.4 us)
Async XLA Ops:
  7.2 823.4 %reduce-scatter.14.cloned.1.call-start = ((), (), s32[]{:S(2)}) async-start(), calls=%async_computation.9 | async-start | bytes 11943936 | tf_op jit(solution)/shard_map/reduce_scatter | solution.py:400
  15.3 56.3 %collective-permute-start.8 = (bf16[288,2304]{1,0:T(8,128)(2,1)S(1)}, bf16[288,2304]{1,0:T(8,128)(2,1)S(1)}, u32[]{:S(2)}, u32[]{:S(2)}) collective-permute-start(bf16[288,2304]{1,0:T(8,128)(2,1)S(1)} %pad_maximum_fusion.1.refs_0_.refs_8_.refs_11_), channel_id=1, source_target_pairs={{0,2},{1,5},{2,0},{3,7},{4,6},{5,1},{6,4},{7,3}} | collective-permute-start | bytes 3981320 | tf_op jit(solution)/shard_map/ppermute | solution.py:35
  15.8 58.4 %collective-permute-start.7 = (bf16[288,2304]{1,0:T(8,128)(2,1)S(1)}, bf16[288,2304]{1,0:T(8,128)(2,1)}, u32[]{:S(2)}, u32[]{:S(2)}) collective-permute-start(bf16[288,2304]{1,0:T(8,128)(2,1)S(1)} %pad_maximum_fusion.1.refs_0_.refs_8_.refs_11_), channel_id=1, source_target_pairs={{0,4},{1,3},{2,6},{3,1},{4,0},{5,7},{6,2},{7,5}} | collective-permute-start | bytes 3981320 | tf_op jit(solution)/shard_map/ppermute | solution.py:35
  45.8 54.2 %collective-permute-start.15 = (bf16[576,1152]{1,0:T(8,128)(2,1)S(1)}, bf16[576,1152]{1,0:T(8,128)(2,1)S(1)}, u32[]{:S(2)}, u32[]{:S(2)}) collective-permute-start(bf16[576,1152]{1,0:T(8,128)(2,1)S(1)} %get-tuple-element.50.refs_0_), channel_id=1, source_target_pairs={{0,2},{1,5},{2,0},{3,7},{4,6},{5,1},{6,4},{7,3}} | collective-permute-start | bytes 3981320 | tf_op jit(solution)/shard_map/ppermute | solution.py:35
  45.9 54.2 %collective-permute-start.14 = (bf16[576,1152]{1,0:T(8,128)(2,1)S(1)}, bf16[576,1152]{1,0:T(8,128)(2,1)S(1)}, u32[]{:S(2)}, u32[]{:S(2)}) collective-permute-start(bf16[576,1152]{1,0:T(8,128)(2,1)S(1)} %get-tuple-element.50.refs_0_), channel_id=1, source_target_pairs={{0,4},{1,3},{2,6},{3,1},{4,0},{5,7},{6,2},{7,5}} | collective-permute-start | bytes 3981320 | tf_op jit(solution)/shard_map/ppermute | solution.py:35
  47.8 54.8 %collective-permute-start.10 = (bf16[288,2304]{1,0:T(8,128)(2,1)S(1)}, bf16[288,2304]{1,0:T(8,128)(2,1)S(1)}, u32[]{:S(2)}, u32[]{:S(2)}) collective-permute-start(bf16[288,2304]{1,0:T(8,128)(2,1)S(1)} %pad_maximum_fusion.1.refs_0_.refs_8_.refs_11_), channel_id=1, source_target_pairs={{0,1},{1,0},{2,3},{3,2},{4,5},{5,4},{6,7},{7,6}} | collective-permute-start | bytes 3981320 | tf_op jit(solution)/shard_map/ppermute | solution.py:35
  102.6 44.4 %collective-permute-start.29 = (bf16[288,2304]{1,0:T(8,128)(2,1)S(1)}, bf16[288,2304]{1,0:T(8,128)(2,1)S(1)}, u32[]{:S(2)}, u32[]{:S(2)}) collective-permute-start(bf16[288,2304]{1,0:T(8,128)(2,1)S(1)} %pad_maximum_fusion.3.refs_0_.refs_8_.refs_11_), channel_id=1, source_target_pairs={{0,2},{1,5},{2,0},{3,7},{4,6},{5,1},{6,4},{7,3}} | collective-permute-start | bytes 3981320 | tf_op jit(solution)/shard_map/ppermute | solution.py:35
  102.6 44.4 %collective-permute-start.28 = (bf16[288,2304]{1,0:T(8,128)(2,1)S(1)}, bf16[288,2304]{1,0:T(8,128)(2,1)S(1)}, u32[]{:S(2)}, u32[]{:S(2)}) collective-permute-start(bf16[288,2304]{1,0:T(8,128)(2,1)S(1)} %pad_maximum_fusion.3.refs_0_.refs_8_.refs_11_), channel_id=1, source_target_pairs={{0,4},{1,3},{2,6},{3,1},{4,0},{5,7},{6,2},{7,5}} | collective-permute-start | bytes 3981320 | tf_op jit(solution)/shard_map/ppermute | solution.py:35
  103.6 57.7 %collective-permute-start.22 = (bf16[288,2304]{1,0:T(8,128)(2,1)}, bf16[288,2304]{1,0:T(8,128)(2,1)}, u32[]{:S(2)}, u32[]{:S(2)}) collective-permute-start(bf16[288,2304]{1,0:T(8,128)(2,1)} %pad_maximum_fusion.2.refs_0_.refs_3_), channel_id=1, source_target_pairs={{0,2},{1,5},{2,0},{3,7},{4,6},{5,1},{6,4},{7,3}} | collective-permute-start | bytes 3981320 | tf_op jit(solution)/shard_map/ppermute | solution.py:35
  105.6 81.4 %collective-permute-start.9 = (bf16[288,2304]{1,0:T(8,128)(2,1)}, bf16[288,2304]{1,0:T(8,128)(2,1)}, u32[]{:S(2)}, u32[]{:S(2)}) collective-permute-start(bf16[288,2304]{1,0:T(8,128)(2,1)} %collective-permute-done.7.refs_1_.refs_9_.refs_12_), channel_id=1, source_target_pairs={{0,2},{1,5},{2,0},{3,7},{4,6},{5,1},{6,4},{7,3}} | collective-permute-start | bytes 3981320 | tf_op jit(solution)/shard_map/ppermute | solution.py:35
  131.8 55.2 %collective-permute-start.5 = (bf16[288,2304]{1,0:T(8,128)(2,1)}, bf16[288,2304]{1,0:T(8,128)(2,1)}, u32[]{:S(2)}, u32[]{:S(2)}) collective-permute-start(bf16[288,2304]{1,0:T(8,128)(2,1)} %collective-permute-done.1.refs_2_.refs_5_), channel_id=1, source_target_pairs={{0,1},{1,0},{2,3},{3,2},{4,5},{5,4},{6,7},{7,6}} | collective-permute-start | bytes 3981320 | tf_op jit(solution)/shard_map/ppermute | solution.py:35
  147.0 40.5 %collective-permute-start.4 = (bf16[288,2304]{1,0:T(8,128)(2,1)}, bf16[288,2304]{1,0:T(8,128)(2,1)}, u32[]{:S(2)}, u32[]{:S(2)}) collective-permute-start(bf16[288,2304]{1,0:T(8,128)(2,1)} %collective-permute-done.refs_1_.refs_4_), channel_id=1, source_target_pairs={{0,1},{1,0},{2,3},{3,2},{4,5},{5,4},{6,7},{7,6}} | collective-permute-start | bytes 3981320 | tf_op jit(solution)/shard_map/ppermute | solution.py:35
  147.0 42.7 %collective-permute-start.6 = (bf16[288,2304]{1,0:T(8,128)(2,1)}, bf16[288,2304]{1,0:T(8,128)(2,1)}, u32[]{:S(2)}, u32[]{:S(2)}) collective-permute-start(bf16[288,2304]{1,0:T(8,128)(2,1)} %collective-permute-done.2.refs_3_.refs_6_), channel_id=1, source_target_pairs={{0,1},{1,0},{2,3},{3,2},{4,5},{5,4},{6,7},{7,6}} | collective-permute-start | bytes 3981320 | tf_op jit(solution)/shard_map/ppermute | solution.py:35
  161.3 62.9 %collective-permute-start.21 = (bf16[288,2304]{1,0:T(8,128)(2,1)}, bf16[288,2304]{1,0:T(8,128)(2,1)}, u32[]{:S(2)}, u32[]{:S(2)}) collective-permute-start(bf16[288,2304]{1,0:T(8,128)(2,1)} %pad_maximum_fusion.2.refs_0_.refs_3_), channel_id=1, source_target_pairs={{0,4},{1,3},{2,6},{3,1},{4,0},{5,7},{6,2},{7,5}} | collective-permute-start | bytes 3981320 | tf_op jit(solution)/shard_map/ppermute | solution.py:35
  186.9 37.9 %collective-permute-start.17 = (bf16[576,1152]{1,0:T(8,128)(2,1)}, bf16[576,1152]{1,0:T(8,128)(2,1)}, u32[]{:S(2)}, u32[]{:S(2)}) collective-permute-start(bf16[576,1152]{1,0:T(8,128)(2,1)} %copy-done.5), channel_id=1, source_target_pairs={{0,1},{1,0},{2,3},{3,2},{4,5},{5,4},{6,7},{7,6}} | collective-permute-start | bytes 3981320 | tf_op jit(solution)/shard_map/ppermute | solution.py:35
  187.5 37.9 %collective-permute-start.16 = (bf16[576,1152]{1,0:T(8,128)(2,1)}, bf16[576,1152]{1,0:T(8,128)(2,1)}, u32[]{:S(2)}, u32[]{:S(2)}) collective-permute-start(bf16[576,1152]{1,0:T(8,128)(2,1)} %copy-done.11), channel_id=1, source_target_pairs={{0,2},{1,5},{2,0},{3,7},{4,6},{5,1},{6,4},{7,3}} | collective-permute-start | bytes 3981320 | tf_op jit(solution)/shard_map/ppermute | solution.py:35
  260.3 41.1 %collective-permute-start.31 = (bf16[288,2304]{1,0:T(8,128)(2,1)}, bf16[288,2304]{1,0:T(8,128)(2,1)}, u32[]{:S(2)}, u32[]{:S(2)}) collective-permute-start(bf16[288,2304]{1,0:T(8,128)(2,1)} %copy-done.4), channel_id=1, source_target_pairs={{0,1},{1,0},{2,3},{3,2},{4,5},{5,4},{6,7},{7,6}} | collective-permute-start | bytes 3981320 | tf_op jit(solution)/shard_map/ppermute | solution.py:35
  260.4 39.9 %collective-permute-start.25 = (bf16[288,2304]{1,0:T(8,128)(2,1)}, bf16[288,2304]{1,0:T(8,128)(2,1)}, u32[]{:S(2)}, u32[]{:S(2)}) collective-permute-start(bf16[288,2304]{1,0:T(8,128)(2,1)} %collective-permute-done.21.refs_1_.refs_4_), channel_id=1, source_target_pairs={{0,1},{1,0},{2,3},{3,2},{4,5},{5,4},{6,7},{7,6}} | collective-permute-start | bytes 3981320 | tf_op jit(solution)/shard_map/ppermute | solution.py:35
  260.9 41.1 %collective-permute-start.35 = (bf16[576,1152]{1,0:T(8,128)(2,1)}, bf16[576,1152]{1,0:T(8,128)(2,1)}, u32[]{:S(2)}, u32[]{:S(2)}) collective-permute-start(bf16[576,1152]{1,0:T(8,128)(2,1)} %get-tuple-element.61.refs_0_), channel_id=1, source_target_pairs={{0,4},{1,3},{2,6},{3,1},{4,0},{5,7},{6,2},{7,5}} | collective-permute-start | bytes 3981320 | tf_op jit(solution)/shard_map/ppermute | solution.py:35
  262.2 40.7 %collective-permute-start.30 = (bf16[288,2304]{1,0:T(8,128)(2,1)}, bf16[288,2304]{1,0:T(8,128)(2,1)}, u32[]{:S(2)}, u32[]{:S(2)}) collective-permute-start(bf16[288,2304]{1,0:T(8,128)(2,1)} %copy-done.14), channel_id=1, source_target_pairs={{0,2},{1,5},{2,0},{3,7},{4,6},{5,1},{6,4},{7,3}} | collective-permute-start | bytes 3981320 | tf_op jit(solution)/shard_map/ppermute | solution.py:35
  263.2 38.8 %collective-permute-start.27 = (bf16[288,2304]{1,0:T(8,128)(2,1)}, bf16[288,2304]{1,0:T(8,128)(2,1)}, u32[]{:S(2)}, u32[]{:S(2)}) collective-permute-start(bf16[288,2304]{1,0:T(8,128)(2,1)} %collective-permute-done.23.refs_3_.refs_6_), channel_id=1, source_target_pairs={{0,1},{1,0},{2,3},{3,2},{4,5},{5,4},{6,7},{7,6}} | collective-permute-start | bytes 3981320 | tf_op jit(solution)/shard_map/ppermute | solution.py:35
  337.4 67.9 %collective-permute-start.38 = (bf16[576,1152]{1,0:T(8,128)(2,1)}, bf16[576,1152]{1,0:T(8,128)(2,1)}, u32[]{:S(2)}, u32[]{:S(2)}) collective-permute-start(bf16[576,1152]{1,0:T(8,128)(2,1)} %get-tuple-element.61.refs_0_), channel_id=1, source_target_pairs={{0,1},{1,0},{2,3},{3,2},{4,5},{5,4},{6,7},{7,6}} | collective-permute-start | bytes 3981320 | tf_op jit(solution)/shard_map/ppermute | solution.py:35
  338.0 67.4 %collective-permute-start.39 = (bf16[576,1152]{1,0:T(8,128)(2,1)}, bf16[576,1152]{1,0:T(8,128)(2,1)}, u32[]{:S(2)}, u32[]{:S(2)}) collective-permute-start(bf16[576,1152]{1,0:T(8,128)(2,1)} %collective-permute-done.35.refs_1_), channel_id=1, source_target_pairs={{0,1},{1,0},{2,3},{3,2},{4,5},{5,4},{6,7},{7,6}} | collective-permute-start | bytes 3981320 | tf_op jit(solution)/shard_map/ppermute | solution.py:35
  338.0 67.4 %collective-permute-start.40 = (bf16[576,1152]{1,0:T(8,128)(2,1)}, bf16[576,1152]{1,0:T(8,128)(2,1)}, u32[]{:S(2)}, u32[]{:S(2)}) collective-permute-start(bf16[576,1152]{1,0:T(8,128)(2,1)} %collective-permute-done.36.refs_2_), channel_id=1, source_target_pairs={{0,1},{1,0},{2,3},{3,2},{4,5},{5,4},{6,7},{7,6}} | collective-permute-start | bytes 3981320 | tf_op jit(solution)/shard_map/ppermute | solution.py:35
  338.5 66.9 %collective-permute-start.41 = (bf16[576,1152]{1,0:T(8,128)(2,1)}, bf16[576,1152]{1,0:T(8,128)(2,1)}, u32[]{:S(2)}, u32[]{:S(2)}) collective-permute-start(bf16[576,1152]{1,0:T(8,128)(2,1)} %collective-permute-done.37.refs_3_), channel_id=1, source_target_pairs={{0,1},{1,0},{2,3},{3,2},{4,5},{5,4},{6,7},{7,6}} | collective-permute-start | bytes 3981320 | tf_op jit(solution)/shard_map/ppermute | solution.py:35
  405.3 425.2 %reduce-scatter.6.cloned.1.call-start = ((), (), s32[]{:S(2)}) async-start(), calls=%async_computation.5 | async-start | bytes 11943936 | tf_op jit(solution)/shard_map/reduce_scatter | solution.py:400
  704.1 184.5 %reduce-scatter.8.cloned.1.call-start = ((), (), s32[]{:S(2)}) async-start(), calls=%async_computation.6 | async-start | bytes 11943936 | tf_op jit(solution)/shard_map/reduce_scatter | solution.py:400
  704.9 261.3 %reduce-scatter.12.cloned.1.call-start = ((), (), s32[]{:S(2)}) async-start(), calls=%async_computation.8 | async-start | bytes 11943936 | tf_op jit(solution)/shard_map/reduce_scatter | solution.py:400
  705.5 338.3 %reduce-scatter.10.cloned.1.call-start = ((), (), s32[]{:S(2)}) async-start(), calls=%async_computation.7 | async-start | bytes 11943936 | tf_op jit(solution)/shard_map/reduce_scatter | solution.py:400
  738.4 39.8 %collective-permute-start.44 = (bf16[288,2304]{1,0:T(8,128)(2,1)}, bf16[288,2304]{1,0:T(8,128)(2,1)}, u32[]{:S(2)}, u32[]{:S(2)}) collective-permute-start(bf16[288,2304]{1,0:T(8,128)(2,1)} %get-tuple-element.89), channel_id=1, source_target_pairs={{0,4},{1,3},{2,6},{3,1},{4,0},{5,7},{6,2},{7,5}} | collective-permute-start | bytes 3981320 | tf_op jit(solution)/shard_map/ppermute | solution.py:35
  776.1 49.0 %collective-permute-start.43 = (bf16[288,2304]{1,0:T(8,128)(2,1)}, bf16[288,2304]{1,0:T(8,128)(2,1)}, u32[]{:S(2)}, u32[]{:S(2)}) collective-permute-start(bf16[288,2304]{1,0:T(8,128)(2,1)} %get-tuple-element.88), channel_id=1, source_target_pairs={{0,4},{1,3},{2,6},{3,1},{4,0},{5,7},{6,2},{7,5}} | collective-permute-start | bytes 3981320 | tf_op jit(solution)/shard_map/ppermute | solution.py:35
  782.7 42.4 %collective-permute-start.45 = (bf16[288,2304]{1,0:T(8,128)(2,1)}, bf16[288,2304]{1,0:T(8,128)(2,1)}, u32[]{:S(2)}, u32[]{:S(2)}) collective-permute-start(bf16[288,2304]{1,0:T(8,128)(2,1)} %fusion), channel_id=1, source_target_pairs={{0,2},{1,5},{2,0},{3,7},{4,6},{5,1},{6,4},{7,3}} | collective-permute-start | bytes 3981320 | tf_op jit(solution)/shard_map/ppermute | solution.py:35
  (34 other events, 1112.0 us)
Sparse Core Ops, SparseCore 0:
  405.4 74.2 reduce-scatter.13
  704.3 105.9 reduce-scatter.5
  813.7 74.8 reduce-scatter.7
  891.9 74.2 reduce-scatter.11
  969.5 74.2 reduce-scatter.9
